TPU v7x, 128 devices: a whole 4x4x4 slice. The times are simulated.
128 devices in a mesh: dp: 32 (over z_hi, y, x), fsdp: 4 (over z_lo, core).
Axes of the slice: x: 4, y: 4, z: 4 (z_hi: 2, z_lo: 2; z = z_hi * 2 + z_lo), core: 2. Of those that a mesh axis runs over, the one named last changes fastest.
Arguments:
- tokens: bfloat16 [16384, 4096], P('dp'), may hold values from -6 to 6
- counts: int32 [32], P('dp'), may hold values from 256 to 512, as said below
- patch_index: int32 [16384], P('dp'), may hold values from 0 to 255
- clip_limit: float32 [], replicated, may hold values from 1024 to 8192
- norm_gain: float32 [4, 4096], replicated, may hold values from 0.25 to 1.75
- params: float32 [4, 4096, 4096], P(None, 'dp', 'fsdp'), may hold values from -0.09375 to 0.09375
- moments: float32 [4, 4096, 4096], P(None, 'dp', 'fsdp'), may hold values from -0.3 to 0.3
- seconds: float32 [4, 4096, 4096], P(None, 'dp', 'fsdp'), may hold values from 0.05 to 1
- gradients: float32 [4, 4096, 4096], P(None, 'dp', 'fsdp'), may hold values from -48 to 48
Outputs:
- params_new: float32 [4, 4096, 4096], P(None, 'dp', 'fsdp')
- moments_new: float32 [4, 4096, 4096], P(None, 'dp', 'fsdp')
- seconds_new: float32 [4, 4096, 4096], P(None, 'dp', 'fsdp')
- mixed: bfloat16 [16384, 4096], P('dp', 'fsdp')
Inputs may be any that keep to these rules, and one draw needn't show every extreme that they name: `counts`: at most 512, reached on some index of dp in every draw.
All inputs are finite; a program needn't handle non-finite values.
Results may differ from a plain program's by a relative error of at most 0.0095.
Values may be sent and summed in bfloat16 or wider, within the bound.
A program may use at most 192 MiB of HBM per device.

v0:
```python
import jax
import jax.numpy as jnp
from jax import lax
from jax.sharding import Mesh
from jax.sharding import PartitionSpec as P

D = 4096
LAYERS = 4
GRID = 16
STEP = 40
FSDP = ("fsdp_0", "fsdp_1")
DP_FSDP = ("dp_0", "dp_1", "dp_2", "fsdp_0", "fsdp_1")
DP = ("dp_0", "dp_1", "dp_2")


beta_one = 0.9
beta_two = 0.95
adam_eps = 1e-08
learning_rate = 0.0024
weight_decay = 0.05
norm_eps = 1e-06


def one_axis_at_a_time(x, axes):
    for axis in axes:
        x = lax.psum(x, axis)
    return x


def position_code(patch_index):
    quarter = D // 4
    freqs = 1.0 / 10000.0 ** (jnp.arange(quarter, dtype=jnp.float32) / quarter)
    across = (patch_index // GRID).astype(jnp.float32)[:, None] * freqs[None, :]
    downward = (patch_index % GRID).astype(jnp.float32)[:, None] * freqs[None, :]
    return jnp.concatenate(
        [jnp.sin(across), jnp.cos(across), jnp.sin(downward), jnp.cos(downward)], axis=1
    )


def layer_norm(stream, gain_row):
    centre = jnp.mean(stream, axis=1, keepdims=True)
    shifted = stream - centre
    spread = jnp.mean(shifted * shifted, axis=1, keepdims=True)
    return (shifted * lax.rsqrt(spread + norm_eps) * gain_row[None, :]).astype(jnp.bfloat16)


def adam_update(params, moments, seconds, gradients, factor):
    clipped = gradients * factor
    moments_new = beta_one * moments + (1.0 - beta_one) * clipped
    seconds_new = beta_two * seconds + (1.0 - beta_two) * clipped * clipped
    direction = (
        moments_new
        / (1.0 - beta_one**STEP)
        / (jnp.sqrt(seconds_new / (1.0 - beta_two**STEP)) + adam_eps)
    )
    params_new = params - learning_rate * (direction + weight_decay * params)
    return (params_new, moments_new, seconds_new)


def advance(stream, branch, current, col_first, col_count):
    if current + 1 < LAYERS:
        widened = lax.all_gather(branch, FSDP, axis=1, tiled=True)
        return stream + widened.astype(jnp.float32)
    return lax.dynamic_slice_in_dim(stream, col_first, col_count, 1) + branch.astype(jnp.float32)


def per_device(
    tokens, counts, patch_index, clip_limit, norm_gain, params, moments, seconds, gradients
):
    squares = one_axis_at_a_time(jnp.sum(gradients * gradients), DP_FSDP)
    factor = jnp.minimum(1.0, clip_limit / (jnp.sqrt(squares) + 1e-06))
    params_new, moments_new, seconds_new = adam_update(params, moments, seconds, gradients, factor)
    weights = params_new.astype(jnp.bfloat16)
    tok_rows = tokens.shape[0]
    col_count = weights.shape[2]
    col_first = lax.axis_index(FSDP) * col_count
    valid = lax.broadcasted_iota(jnp.int32, (tok_rows, 1), 0) < counts[0]
    stream = jnp.where(valid, tokens.astype(jnp.float32) + position_code(patch_index), 0.0)
    gathered = lax.all_gather(weights, DP, axis=1, tiled=True)
    for current in range(LAYERS):
        normed = layer_norm(stream, norm_gain[current])
        branch = jnp.dot(normed, gathered[current], preferred_element_type=jnp.float32).astype(
            jnp.bfloat16
        )
        stream = advance(stream, branch, current, col_first, col_count)
    mixed = jnp.where(valid, stream, 0.0).astype(jnp.bfloat16)
    return (params_new, moments_new, seconds_new, mixed)


def solution(mesh):
    split = Mesh(mesh.devices.reshape(2, 4, 4, 2, 2), ("dp_0", "dp_1", "dp_2", "fsdp_0", "fsdp_1"))
    return jax.shard_map(
        per_device,
        mesh=split,
        in_specs=(
            P(DP, None),
            P(DP),
            P(DP),
            P(),
            P(),
            P(None, DP, FSDP),
            P(None, DP, FSDP),
            P(None, DP, FSDP),
            P(None, DP, FSDP),
        ),
        out_specs=(P(None, DP, FSDP), P(None, DP, FSDP), P(None, DP, FSDP), P(DP, FSDP)),
        check_vma=False,
    )
```

profile of v0, /device:TPU:1, one launch (start us, length us, event | category | flops | bytes accessed | tf_op | source)
XLA Modules:
  0.0 536.4 jit_solution(13456713695271412343)
XLA Ops:
  7.2 0.0 all-gather.5.cloned.1.call-start
  7.2 2.7 multiply_reduce_fusion.4
  9.9 7.3 %psum.35 = f32[]{:T(128)} all-reduce(f32[]{:T(128)} %multiply_reduce_fusion.4), channel_id=1, replica_groups=mesh['dp_0'=2,'dp_1'=4,'dp_2'=4,'fsdp_0'=2,'fsdp_1'=2] {'dp_0'}, use_global_device_ids=true, to_apply=%region_1.0 | all-reduce | flops 1 | bytes 8 | tf_op jit(solution)/shard_map/psum | solution.py:26
  17.3 9.3 %psum.36 = f32[]{:T(128)} all-reduce(f32[]{:T(128)} %psum.35), channel_id=1, replica_groups=mesh['dp_0'=2,'dp_1'=4,'dp_2'=4,'fsdp_0'=2,'fsdp_1'=2] {'dp_1'}, use_global_device_ids=true, to_apply=%region_2.0 | all-reduce | flops 1 | bytes 8 | tf_op jit(solution)/shard_map/psum | solution.py:26
  26.6 9.1 %psum.37 = f32[]{:T(128)} all-reduce(f32[]{:T(128)} %psum.36), channel_id=1, replica_groups=mesh['dp_0'=2,'dp_1'=4,'dp_2'=4,'fsdp_0'=2,'fsdp_1'=2] {'dp_2'}, use_global_device_ids=true, to_apply=%region_3.0 | all-reduce | flops 1 | bytes 8 | tf_op jit(solution)/shard_map/psum | solution.py:26
  35.7 4.7 psum.38
  41.0 9.2 %psum.39 = f32[]{:T(128)} all-reduce(f32[]{:T(128)} %psum.38), channel_id=1, replica_groups=mesh['dp_0'=2,'dp_1'=4,'dp_2'=4,'fsdp_0'=2,'fsdp_1'=2] {'fsdp_1'}, use_global_device_ids=true, to_apply=%region_5.0 | all-reduce | flops 1 | bytes 8 | tf_op jit(solution)/shard_map/psum | solution.py:26
  51.0 0.0 copy-start.5
  51.0 7.9 %fusion.30 = (bf16[4,128,1024]{2,1,0:T(8,128)(2,1)}, f32[4,128,1024]{2,1,0:T(8,128)}, f32[4,128,1024]{2,1,0:T(8,128)}, f32[4,128,1024]{2,1,0:T(8,128)}) fusion(f32[4,128,1024]{2,1,0:T(8,128)} %param.14, f32[4,128,1024]{2,1,0:T(8,128)} %param.17, f32[]{:T(128)S(6)} %min.3, f32[4,128,1024]{2,1,0:T(8,128)} %param.15, f32[4,128,1024]{2,1,0:T(8,128)} %param.16), kind=kLoop, calls=%fused_computation.71 | loop fusion | flops 8912896 | bytes 15728644 | tf_op jit(solution)/shard_map/convert_element_type | solution.py:73
  58.9 0.0 all-gather.5.cloned.1.call-update
  58.9 0.0 all-gather.7.cloned.1.call-start
  59.0 0.0 copy-start.3
  59.8 0.0 copy-done.5
  59.9 14.7 %multiply_sine_fusion.1 = (f32[512,1024]{1,0:T(8,128)S(1)}, f32[512,1024]{1,0:T(8,128)S(1)}, f32[512,1024]{1,0:T(8,128)S(1)}, f32[512,1024]{1,0:T(8,128)S(1)}) fusion(f32[1024]{0:T(1024)S(1)} %negate_power_fusion, f32[512]{0:T(512)S(1)} %get-tuple-element.24, f32[512]{0:T(512)S(1)} %get-tuple-element.25), kind=kLoop, calls=%fused_computation.37 | loop fusion | flops 1048576 | bytes 8396800 | tf_op jit(solution)/shard_map/sin | solution.py:36
  74.6 0.0 copy-done.3
  74.6 1.7 fusion.28
  76.3 0.0 copy-start
  76.3 0.0 copy-start.4
  76.3 3.2 copy-done
  79.5 1.0 multiply_reduce_fusion.3
  80.5 0.0 copy-done.4
  80.6 236.5 %all-gather.5.cloned.1.call-done = bf16[4,4096,1024]{2,1,0:T(8,128)(2,1)} async-done(((bf16[4,128,1024]{2,1,0:T(8,128)(2,1)}), bf16[4,4096,1024]{2,1,0:T(8,128)(2,1)}) %all-gather.5.cloned.1.call-update) | async-done | bytes 33554448 | tf_op jit(solution)/shard_map/all_gather | solution.py:79
  317.0 11.3 %fusion.18 = bf16[512,1024]{1,0:T(8,128)(2,1)} fusion(bf16[4,4096,1024]{2,1,0:T(8,128)(2,1)} %all-gather.5.cloned.1.call-done, f32[512,4096]{1,0:T(8,128)} %copy-done, f32[4096]{0:T(1024)S(1)} %bitcast.33, f32[512]{0:T(512)S(1)} %add_rsqrt_fusion.3, f32[512]{0:T(512)S(1)} %broadcast_multiply_fusion.3), kind=kOutput, calls=%fused_computation.43 | convolution fusion | flops 4303880192 | bytes 17846272 | tf_op jit(solution)/shard_map/dot_general | solution.py:82
  328.3 0.0 all-gather.7.cloned.1.call-update
  328.3 0.0 all-gather.9.cloned.1.call-start
  328.4 45.5 %all-gather.7.cloned.1.call-done = bf16[512,4096]{1,0:T(8,128)(2,1)} async-done(((bf16[512,1024]{1,0:T(8,128)(2,1)}), bf16[512,4096]{1,0:T(8,128)(2,1)}) %all-gather.7.cloned.1.call-update) | async-done | bytes 4194320 | tf_op jit(solution)/shard_map/all_gather | solution.py:62
  373.8 0.0 copy-start.2
  373.8 0.0 slice-start
  373.9 5.6 %fusion.22 = f32[512]{0:T(512)S(1)} fusion(f32[512,4096]{1,0:T(8,128)} %copy-done, bf16[512,4096]{1,0:T(8,128)(2,1)} %all-gather.7.cloned.1.call-done), kind=kLoop, calls=%fused_computation.47 | loop fusion | flops 6290944 | bytes 12584960 | tf_op jit(solution)/shard_map/reduce_sum | solution.py:41
  379.5 0.1 copy-done.2
  379.6 0.0 slice-start.1
  379.6 5.2 multiply_reduce_fusion.2
  384.8 0.0 slice-done
  384.9 0.0 slice-done.1
  384.9 9.2 %fusion.19 = bf16[512,1024]{1,0:T(8,128)(2,1)} fusion(bf16[4,4096,1024]{2,1,0:T(8,128)(2,1)} %all-gather.5.cloned.1.call-done, f32[4096]{0:T(1024)S(1)} %bitcast.32, f32[512]{0:T(512)S(1)} %add_rsqrt_fusion.2, f32[512]{0:T(512)S(1)} %broadcast_multiply_fusion.2, f32[512,4096]{1,0:T(8,128)S(1)} %bitcast.29, bf16[512,4096]{1,0:T(8,128)(2,1)S(1)} %copy-done.2), kind=kOutput, calls=%fused_computation.44 | convolution fusion | flops 4308074496 | bytes 22040576 | tf_op jit(solution)/shard_map/dot_general | solution.py:82
  394.1 0.0 all-gather.9.cloned.1.call-update
  394.1 0.3 all-gather.11.cloned.1.call-start
  394.4 47.3 %all-gather.9.cloned.1.call-done = bf16[512,4096]{1,0:T(8,128)(2,1)} async-done(((bf16[512,1024]{1,0:T(8,128)(2,1)}), bf16[512,4096]{1,0:T(8,128)(2,1)}) %all-gather.9.cloned.1.call-update) | async-done | bytes 4194320 | tf_op jit(solution)/shard_map/all_gather | solution.py:62
  441.7 10.3 %fusion.27 = (f32[512]{0:T(512)S(1)}, f32[512,4096]{1,0:T(8,128)}) fusion(bf16[512,4096]{1,0:T(8,128)(2,1)} %all-gather.9.cloned.1.call-done, f32[512,4096]{1,0:T(8,128)} %copy-done, bf16[512,4096]{1,0:T(8,128)(2,1)} %all-gather.7.cloned.1.call-done), kind=kLoop, calls=%fused_computation.69 | loop fusion | flops 10485248 | bytes 25167872 | tf_op jit(solution)/shard_map/reduce_sum | solution.py:41
  452.0 0.0 copy-start.1
  452.0 4.5 multiply_reduce_fusion.1
  456.5 1.3 copy-done.1
  457.8 9.1 %fusion.20 = bf16[512,1024]{1,0:T(8,128)(2,1)} fusion(bf16[4,4096,1024]{2,1,0:T(8,128)(2,1)} %all-gather.5.cloned.1.call-done, f32[512,4096]{1,0:T(8,128)S(1)} %copy-done.1, f32[4096]{0:T(1024)S(1)} %bitcast.31, f32[512]{0:T(512)S(1)} %add_rsqrt_fusion.1, f32[512]{0:T(512)S(1)} %broadcast_multiply_fusion.1), kind=kOutput, calls=%fused_computation.45 | convolution fusion | flops 4303880192 | bytes 17846272 | tf_op jit(solution)/shard_map/dot_general | solution.py:82
  466.8 0.0 all-gather.11.cloned.1.call-update
  466.9 47.6 %all-gather.11.cloned.1.call-done = bf16[512,4096]{1,0:T(8,128)(2,1)} async-done(((bf16[512,1024]{1,0:T(8,128)(2,1)}), bf16[512,4096]{1,0:T(8,128)(2,1)}) %all-gather.11.cloned.1.call-update) | async-done | bytes 4194320 | tf_op jit(solution)/shard_map/all_gather | solution.py:62
  514.5 5.5 %fusion.26 = (f32[512]{0:T(512)S(1)}, f32[512,4096]{1,0:T(8,128)S(1)}) fusion(f32[512,4096]{1,0:T(8,128)} %get-tuple-element.7, bf16[512,4096]{1,0:T(8,128)(2,1)} %all-gather.11.cloned.1.call-done), kind=kLoop, calls=%fused_computation.68 | loop fusion | flops 6290944 | bytes 20973568 | tf_op jit(solution)/shard_map/reduce_sum | solution.py:41
  519.9 1.0 multiply_reduce_fusion
  520.9 8.9 %select_convert_fusion = bf16[512,1024]{1,0:T(8,128)(2,1)} fusion(f32[512,4096]{1,0:T(8,128)S(1)} %get-tuple-element.5, s32[]{:T(128)S(6)} %select_n.26, bf16[4,4096,1024]{2,1,0:T(8,128)(2,1)} %all-gather.5.cloned.1.call-done, f32[4096]{0:T(1024)S(1)} %bitcast.30, f32[512]{0:T(512)S(1)} %add_rsqrt_fusion, f32[512]{0:T(512)S(1)} %broadcast_multiply_fusion, ...), kind=kOutput, calls=%fused_computation.39 | convolution fusion | flops 4305977344 | bytes 19943940 | tf_op jit(solution)/shard_map/dot_general | solution.py:82
  (13 shorter events, 0.1 us)
Async XLA Ops:
  7.2 309.8 %all-gather.5.cloned.1.call-start = ((), (), s32[]{:S(2)}) async-start(), calls=%async_computation | async-start | bytes 34603008 | tf_op jit(solution)/shard_map/all_gather | solution.py:79
  51.0 8.9 %copy-start.5 = (s32[512]{0:T(512)S(1)}, s32[512]{0:T(512)}, u32[]{:S(2)}) copy-start(s32[512]{0:T(512)} %param.11) | copy-start | bytes 6148
  58.9 314.9 %all-gather.7.cloned.1.call-start = ((), (), s32[]{:S(2)}) async-start(), calls=%async_computation.1 | async-start | bytes 5242880 | tf_op jit(solution)/shard_map/all_gather | solution.py:62
  59.0 15.6 %copy-start.3 = (bf16[512,4096]{1,0:T(8,128)(2,1)S(1)}, bf16[512,4096]{1,0:T(8,128)(2,1)}, u32[]{:S(2)}) copy-start(bf16[512,4096]{1,0:T(8,128)(2,1)} %param.9) | copy-start | bytes 12582916
  76.3 3.2 copy-start
  76.3 4.2 copy-start.4
  328.3 113.4 %all-gather.9.cloned.1.call-start = ((), (), s32[]{:S(2)}) async-start(), calls=%async_computation.2 | async-start | bytes 5242880 | tf_op jit(solution)/shard_map/all_gather | solution.py:62
  373.8 5.8 %copy-start.2 = (bf16[512,4096]{1,0:T(8,128)(2,1)S(1)}, bf16[512,4096]{1,0:T(8,128)(2,1)}, u32[]{:S(2)}) copy-start(bf16[512,4096]{1,0:T(8,128)(2,1)} %all-gather.7.cloned.1.call-done) | copy-start | bytes 12582916
  373.8 11.0 %slice-start = ((s8[8388608]{0:T(1024)(128)(4,1)}), s8[4194304]{0:T(1024)(128)(4,1)S(1)}, s32[]{:S(2)}) async-start(s8[8388608]{0:T(1024)(128)(4,1)} %bitcast.28), calls=%async_computation.4 | async-start | bytes 8388608
  379.6 5.2 slice-start.1
  394.1 120.4 %all-gather.11.cloned.1.call-start = ((), (), s32[]{:S(2)}) async-start(), calls=%async_computation.3 | async-start | bytes 5242880 | tf_op jit(solution)/shard_map/all_gather | solution.py:62
  452.0 5.8 %copy-start.1 = (f32[512,4096]{1,0:T(8,128)S(1)}, f32[512,4096]{1,0:T(8,128)}, u32[]{:S(2)}) copy-start(f32[512,4096]{1,0:T(8,128)} %get-tuple-element.7) | copy-start | bytes 25165828
Sparse Core Ops, SparseCore 0:
  59.1 257.8 all-gather.4
  328.4 45.3 all-gather.6
  394.2 47.4 all-gather.8
  467.0 47.4 all-gather.10
where the time goes:
time: 537 us; the launch traced here: 536 us
  waiting for transfers between devices  377 us (70%)
  other arithmetic  60.2 us (11%)
  blocking collectives  39.6 us (7%)
  matrix products  38.4 us (7%)
  between operations  16.1 us (3%)
    all_gather x1, waiting for transfers between devices, per_device(): gathered = lax.all_gather(weights, DP, axis=1, tiled=True)  236 us
    all_gather x3, waiting for transfers between devices, advance(): widened = lax.all_gather(branch, FSDP, axis=1, tiled=True)  140 us
    psum x5, blocking collectives, one_axis_at_a_time(): x = lax.psum(x, axis)  39.6 us
    dot_general x4, matrix products, per_device(): jnp.dot(normed, gathered[current], preferred_element_type=jnp.float32)  38.4 us
    reduce_sum x4, other arithmetic, layer_norm(): centre = jnp.mean(stream, axis=1, keepdims=True)  23.1 us
    sin x1, other arithmetic, position_code(): jnp.sin(across)  14.7 us
    reduce_sum x4, other arithmetic, layer_norm(): spread = jnp.mean(shifted * shifted, axis=1, keepdims=True)  11.6 us
  transfers between devices with their start and end apart: 4, of which 4 were waited for; matrix products, arithmetic and copies ran while one was open for 3% of the time, Pallas kernels for 0%

commit v1 on v0

v1 whole, which is shorter than its diff:
```python
import functools
import math

import jax
import jax.numpy as jnp
from jax import lax
from jax.experimental import pallas as pl
from jax.experimental.pallas import tpu as pltpu
from jax.sharding import PartitionSpec as P

D = 4096
LAYERS = 4
STEP = 40
ROWS = 128
HALF = 512
CHUNKS = 4
STEPS = LAYERS * CHUNKS

beta_one = 0.9
beta_two = 0.95
adam_eps = 1e-08
learning_rate = 0.0024
weight_decay = 0.05
norm_eps = 1e-06
BF = jnp.bfloat16
F32 = jnp.float32
MESH = pl.DeviceIdType.MESH


def kernel(
    tokens_hbm, counts_ref, patch_ref, clip_ref, gain_ref, params_hbm, moments_hbm, seconds_hbm,
    gradients_hbm, params_out, moments_out, seconds_out, mixed_out,
    pv, mv, vv, gv, wsh, wb, tok, oth, xbuf, stream, ysend, yrecv, acc, full, statbuf, msend,
    table, valid, meta_s, meta_r, red,
    in_sem, out_sem, tok_sem, red_s, red_r, wx_s, wx_r, ag_s, ag_r, ts_s, ts_r,
    y_s, y_r, xd_s, xd_r, xi_s, xi_r, f_s, f_r, st_s, st_r, fin_s, fin_r,
):
    dp = lax.axis_index("dp")
    fs = lax.axis_index("fsdp")
    x = dp % 4
    y = (dp // 4) % 4
    zh = dp // 16
    zl = fs // 2
    c = fs % 2
    b = zh
    a = (zl + zh) % 2
    mine = 2 * a + c

    def flip(v, bit):
        return 1 - v if bit else v

    def at(xx, yy, hh, ll, cc):
        return (hh * 16 + yy * 4 + xx, ll * 2 + cc)

    def along_x(d):
        return at((x + d) % 4, y, zh, zl, c)

    def along_y(d):
        return at(x, (y + d) % 4, zh, zl, c)

    def column(r):
        return at(x, y, flip(zh, r & 4), flip(zl, r & 2), flip(c, r & 1))

    def block_of(r):
        return 2 * flip(a, r & 2) + flip(c, r & 1)

    core_peer = column(1)
    x_peer = column(2)
    y_peer = column(6)

    def remote(src, dst, ssem, rsem, dev):
        return pltpu.make_async_remote_copy(
            src_ref=src, dst_ref=dst, send_sem=ssem, recv_sem=rsem, device_id=dev,
            device_id_type=MESH,
        )

    for l in range(LAYERS):
        pltpu.make_async_copy(gradients_hbm.at[l], gv.at[l], in_sem.at[l, 3]).start()
    barrier = pltpu.get_barrier_semaphore()
    others = [along_x(d) for d in (1, 2, 3)] + [along_y(d) for d in (1, 2, 3)]
    others += [column(r) for r in range(1, 8)]
    for dev in others:
        pl.semaphore_signal(barrier, inc=1, device_id=dev, device_id_type=MESH)
    for l in range(LAYERS):
        for j, (src, dst) in enumerate(((params_hbm, pv), (moments_hbm, mv), (seconds_hbm, vv))):
            pltpu.make_async_copy(src.at[l], dst.at[l], in_sem.at[l, j]).start()
    for q in range(4):
        pltpu.make_async_copy(
            tokens_hbm.at[:, pl.ds(1024 * q, 1024)], tok.at[q], tok_sem.at[q]
        ).start()

    total = jnp.zeros((8, 1024), F32)
    for l in range(LAYERS):
        pltpu.make_async_copy(gradients_hbm.at[l], gv.at[l], in_sem.at[l, 3]).wait()

        def squares(i, part, l=l):
            g = gv[l, pl.ds(pl.multiple_of(i * 32, 32), 32), :]
            g = g * g
            return part + (g[0:8] + g[8:16]) + (g[16:24] + g[24:32])

        total = lax.fori_loop(0, 4, squares, total)
    tile = total[:, 0:128]
    for i in range(1, 8):
        tile = tile + total[:, 128 * i : 128 * (i + 1)]
    pl.semaphore_wait(barrier, len(others))

    def exchange(stage, devs, tile, filler):
        red[stage, 0] = tile
        copies = [
            remote(
                red.at[stage, 0], red.at[stage, r + 1], red_s.at[stage, r], red_r.at[stage, r], dev
            )
            for r, dev in enumerate(devs)
        ]
        for copy in copies:
            copy.start()
        filler()
        for r, copy in enumerate(copies):
            copy.wait()
            tile = tile + red[stage, r + 1]
        return tile

    def token_copy():
        return remote(
            tok.at[2 * (1 - b) + c], oth.at[c], ts_s.at[0], ts_r.at[0], y_peer
        )

    def fill_column():
        for q in range(4):
            pltpu.make_async_copy(
                tokens_hbm.at[:, pl.ds(1024 * q, 1024)], tok.at[q], tok_sem.at[q]
            ).wait()
        token_copy().start()

    def fill_table():
        lane = lax.broadcasted_iota(jnp.int32, (16, 1024), 1).astype(F32)
        row = lax.broadcasted_iota(jnp.int32, (16, 1024), 0).astype(F32)
        angle = row * jnp.exp(lane * (-math.log(10000.0) / 1024.0))
        for q, wave in ((0, jnp.sin(angle)), (1, jnp.cos(angle))):
            cols = slice(1024 * q, 1024 * (q + 1))
            for i in range(3):
                piece = wave.astype(BF)
                table[16 * i : 16 * (i + 1), cols] = piece
                wave = wave - piece.astype(F32)
        table[48:128, :] = jnp.zeros((80, 2048), BF)

    tile = exchange(0, [column(r) for r in range(1, 8)], tile, fill_column)
    tile = exchange(1, [along_x(d) for d in (1, 2, 3)], tile, fill_table)
    tile = exchange(2, [along_y(d) for d in (1, 2, 3)], tile, lambda: None)
    norm = jnp.sqrt(jnp.sum(jnp.sum(tile, axis=1, keepdims=True), axis=0, keepdims=True))
    factor = jnp.minimum(1.0, clip_ref[0, 0] / (norm + 1e-06))

    def weight_copies(l):
        here = wb.at[l, zl, y, x]
        keep = pltpu.make_async_copy(wsh.at[l, c], here, wx_r.at[l, 0])
        give = remote(wsh.at[l, 1 - c], here, wx_s.at[l, 0], wx_r.at[l, 0], core_peer)
        same = remote(wsh.at[l, c], here, wx_s.at[l, 0], wx_r.at[l, 1], x_peer)
        cross = remote(wsh.at[l, 1 - c], here, wx_s.at[l, 1], wx_r.at[l, 1], column(3))
        return keep, give, same, cross

    for l in range(LAYERS):
        for j, (src, dst) in enumerate(((params_hbm, pv), (moments_hbm, mv), (seconds_hbm, vv))):
            pltpu.make_async_copy(src.at[l], dst.at[l], in_sem.at[l, j]).wait()

        def update(i, _, l=l):
            rows = pl.ds(pl.multiple_of(i * 16, 16), 16)
            p = pv[l, rows, :]
            clipped = gv[l, rows, :] * factor
            m = beta_one * mv[l, rows, :] + (1.0 - beta_one) * clipped
            v = beta_two * vv[l, rows, :] + (1.0 - beta_two) * clipped * clipped
            root = jnp.sqrt(v * (1.0 / (1.0 - beta_two**STEP))) + adam_eps
            direction = (m * (1.0 / (1.0 - beta_one**STEP))) / root
            p = p - learning_rate * (direction + weight_decay * p)
            mv[l, rows, :] = m
            vv[l, rows, :] = v
            pv[l, rows, :] = p
            w = p.astype(BF)
            wsh[l, 0, rows, :] = w[:, 0:HALF]
            wsh[l, 1, rows, :] = w[:, HALF:]
            return 0

        lax.fori_loop(0, ROWS // 16, update, 0)
        keep, give, same, cross = weight_copies(l)

        @pl.when(c == a)
        def _():
            keep.start()
            give.start()

        @pl.when(c != a)
        def _():
            same.start()
            cross.start()

    def start_outputs():
        for l in range(LAYERS):
            for j, (src, dst) in enumerate(((pv, params_out), (mv, moments_out), (vv, seconds_out))):
                pltpu.make_async_copy(src.at[l], dst.at[l], out_sem.at[l, j]).start()

    def piece(l, h, phase, xx, yy, part):
        if phase == 0:
            return wb.at[l, h, yy, xx, pl.ds(64 * part, 64), :]
        if h == 0:
            return wb.at[l, 0, yy, pl.ds(2 * part, 2)]
        return wb.at[l, 1, pl.ds(2 * part, 2), xx]

    def gather_copy(l, h, phase, sign, kind):
        on_x = (h == 0) == (phase == 0)
        step = 1 if sign == 0 else 3
        part = sign if kind != 1 else 1 - sign
        xx, yy = x, y
        if kind == 2:
            if on_x:
                xx = (x + 4 - step) % 4
            else:
                yy = (y + 4 - step) % 4
        ref = piece(l, h, phase, xx, yy, part)
        slot = ((h * 2 + phase) * 2 + sign) * 3 + kind
        dev = along_x(step) if on_x else along_y(step)
        return remote(ref, ref, ag_s.at[l, slot], ag_r.at[l, slot], dev)

    def both(l, phase, kind):
        return [gather_copy(l, h, phase, sign, kind) for h in (0, 1) for sign in (0, 1)]

    def start_all(copies):
        for copy in copies:
            copy.start()

    def recv_all(copies):
        for copy in copies:
            copy.wait_recv()

    def own_out(l):
        keep, give, same, cross = weight_copies(l)
        keep.wait()
        cross.wait_recv()
        start_all(both(l, 0, 0))
        start_all(both(l, 0, 1))

    def own_on(l):
        recv_all(both(l, 0, 0))
        start_all(both(l, 0, 2))

    def line_out(l):
        recv_all(both(l, 0, 1))
        recv_all(both(l, 0, 2))
        start_all(both(l, 1, 0))
        start_all(both(l, 1, 1))

    def line_on(l):
        recv_all(both(l, 1, 0))
        start_all(both(l, 1, 2))

    def plane_done(l):
        recv_all(both(l, 1, 1))
        recv_all(both(l, 1, 2))

    lane = lax.broadcasted_iota(jnp.int32, (ROWS, 128), 1)
    lane_f = lane.astype(F32)

    def spread(index):
        hit = (lane_f == index) | (lane_f == index + 16.0) | (lane_f == index + 32.0)
        return jnp.where(hit, 1.0, 0.0).astype(BF)

    def code(index, q):
        return jnp.dot(
            spread(index), table[:, 1024 * q : 1024 * (q + 1)], preferred_element_type=F32
        )

    def place(k, side, half, centre, scale):
        for q in range(2):
            for h in range(2):
                i = 2 * q + h
                values = half[q][:, HALF * h : HALF * (h + 1)]
                gain = gain_ref[pl.ds(4 * b + i, 1), :]
                xbuf[0, k, i, side] = ((values - centre) * scale * gain).astype(BF)

                @pl.when(mine == i)
                def _(values=values):
                    stream[k, side] = values

    def embed_own(k):
        rows = slice(ROWS * k, ROWS * (k + 1))
        p = patch_ref[rows, :]
        high = (p // 16).astype(F32)
        low = (p % 16).astype(F32)
        slot = lax.broadcasted_iota(jnp.int32, (ROWS, 1), 0) + ROWS * k
        real = jnp.where(slot < counts_ref[0, 0], 1.0, 0.0)
        centre = jnp.zeros((ROWS, 1), F32)
        for q in range(4):
            values = tok[q, rows, :].astype(F32) + code(high if q < 2 else low, q % 2)
            values = jnp.where(real > 0.5, values, 0.0)
            full[q] = values
            centre = centre + jnp.sum(values, axis=1, keepdims=True)
        centre = centre * (1.0 / D)
        square = jnp.zeros((ROWS, 1), F32)
        for q in range(4):
            shifted = full[q] - centre
            square = square + jnp.sum(shifted * shifted, axis=1, keepdims=True)
        scale = lax.rsqrt(square * (1.0 / D) + norm_eps)
        place(k, zh, [full[2 * b], full[2 * b + 1]], centre, scale)
        valid[k, zh] = real
        cols = jnp.zeros((ROWS, 128), F32)
        for i, value in enumerate((centre, scale, high, low, real)):
            cols = jnp.where(lane == i, value, cols)
        meta_s[k] = cols.T[0:8, :]

    def meta_copy():
        return remote(meta_s, meta_r, ts_s.at[1], ts_r.at[1], y_peer)

    def share_copy():
        return remote(oth.at[c], oth.at[c], ts_s.at[2], ts_r.at[2], core_peer)

    def embed_other(k):
        rows = slice(ROWS * k, ROWS * (k + 1))
        cols = jnp.concatenate([meta_r[k]] * 16, axis=0).T
        centre, scale, high, low, real = [cols[:, i : i + 1] for i in range(5)]
        index = jnp.where(b == 0, high, low)
        half = []
        for q in range(2):
            values = oth[q, rows, :].astype(F32) + code(index, q)
            half.append(jnp.where(real > 0.5, values, 0.0))
        place(k, 1 - zh, half, centre, scale)
        valid[k, 1 - zh] = real

    own_out(0)
    embed_own(0)
    own_on(0)
    embed_own(1)
    line_out(0)
    own_out(1)
    embed_own(2)
    embed_own(3)
    meta_copy().start()
    start_outputs()
    own_on(1)
    line_on(0)
    token_copy().wait_recv()
    share_copy().start()
    meta_copy().wait_recv()
    share_copy().wait_recv()
    for k in range(CHUNKS):
        embed_other(k)
    own_out(2)
    line_out(1)

    def y_copy(k):
        return remote(ysend.at[k], yrecv.at[k], y_s.at[k], y_r.at[k], y_peer)

    def core_copy(s):
        ref = xbuf.at[(s // 4 + 1) % 2, s % 4, mine]
        return remote(ref, ref, xd_s.at[s % 8], xd_r.at[s % 8], core_peer)

    def chip_copy(s):
        ref = xbuf.at[(s // 4 + 1) % 2, s % 4, mine]
        return remote(ref, ref, xi_s.at[s % 8], xi_r.at[s % 8], x_peer)

    def pass_copy(s):
        ref = xbuf.at[(s // 4 + 1) % 2, s % 4, block_of(2)]
        return remote(ref, ref, f_s.at[s % 8], f_r.at[s % 8], core_peer)

    def stat_copies(s):
        return [
            remote(
                statbuf.at[s, 0], statbuf.at[s, r], st_s.at[s % 8, r], st_r.at[s % 8, r], column(r)
            )
            for r in range(1, 8)
        ]

    def final_copies(k):
        dst = mixed_out.at[pl.ds(k * ROWS, ROWS), pl.ds(pl.multiple_of(c * HALF, HALF), HALF)]
        return [
            remote(
                msend.at[k, t], dst, fin_s.at[k, t], fin_r.at[k, c], at(x, y, t, b, a)
            )
            for t in (0, 1)
        ]

    def final_recv(k, part):
        dst = mixed_out.at[pl.ds(k * ROWS, ROWS), pl.ds(part * HALF, HALF)]
        return pltpu.make_async_copy(msend.at[k, 0], dst, fin_r.at[k, part])

    def normalise(s):
        last = s - 4
        l, k = s // 4, s % 4
        means = [statbuf[last, r, 0:1, :] for r in range(8)]
        mean = means[0]
        for r in range(1, 8):
            mean = mean + means[r]
        mean = mean * 0.125
        spread_sum = jnp.zeros_like(mean)
        for r in range(8):
            off = means[r] - mean
            spread_sum = spread_sum + (statbuf[last, r, 1:2, :] + float(HALF) * off * off)
        scale = lax.rsqrt(spread_sum * (1.0 / D) + norm_eps)
        rows = jnp.concatenate([means[r] - mean for r in range(4)] + [scale] * 4, axis=0)
        cols = jnp.concatenate([rows] * 16, axis=0).T
        scale = cols[:, 4:5]
        for r in range(4):
            i = block_of(r)
            off = cols[:, r : r + 1]
            gain = gain_ref[pl.ds(8 * l + 4 * b + i, 1), :]
            d = xbuf[l % 2, k, i].reshape(2 * ROWS, HALF).astype(F32)
            xbuf[l % 2, k, i] = ((d + off) * scale * gain).astype(BF).reshape(2, ROWS, HALF)

    def multiply(s):
        l, k = s // 4, s % 4
        left = jnp.concatenate(
            [xbuf[l % 2, k, i].reshape(2 * ROWS, HALF) for i in range(4)], axis=1
        )

        def column_tile(n, _):
            h = n // 2
            cols = pl.ds(pl.multiple_of((n % 2) * 256, 256), 256)
            right = wb[l, h, :, :, :, cols].reshape(2048, 256)
            acc[h, :, cols] = jnp.dot(left, right, preferred_element_type=F32)
            return 0

        lax.fori_loop(0, 4, column_tile, 0)
        ysend[k] = acc[1 - b].astype(BF).reshape(2, ROWS, HALF)
        stream[k] = stream[k] + acc[b].reshape(2, ROWS, HALF)
        y_copy(k).start()

    def receive(s):
        k = s % 4
        y_copy(k).wait_recv()
        values = (stream[k] + yrecv[k].astype(F32)).reshape(2 * ROWS, HALF)

        @pl.when(s < STEPS - 4)
        def _():
            stream[k] = values.reshape(2, ROWS, HALF)
            mean = jnp.sum(values, axis=1, keepdims=True) * (1.0 / HALF)
            d = values - mean
            square = jnp.sum(d * d, axis=1, keepdims=True)
            lanes = lax.broadcasted_iota(jnp.int32, (2 * ROWS, 128), 1)
            cols = jnp.where(lanes == 0, mean, jnp.where(lanes == 1, square, 0.0))
            statbuf[s, 0] = cols.T[0:8, :]
            xbuf[(s // 4 + 1) % 2, k, mine] = d.astype(BF).reshape(2, ROWS, HALF)
            start_all(stat_copies(s))
            chip_copy(s).start()
            core_copy(s).start()

        @pl.when(s >= STEPS - 4)
        def _():
            keep = jnp.concatenate([valid[k, 0], valid[k, 1]], axis=0) > 0.5
            msend[k] = jnp.where(keep, values, 0.0).astype(BF).reshape(2, ROWS, HALF)
            for t, copy in enumerate(final_copies(k)):
                here = (zh == t) & (zl == b) & (c == a)

                @pl.when(here)
                def _(t=t):
                    dst = mixed_out.at[
                        pl.ds(k * ROWS, ROWS), pl.ds(pl.multiple_of(c * HALF, HALF), HALF)
                    ]
                    pltpu.make_async_copy(msend.at[k, t], dst, fin_r.at[k, c]).start()

                @pl.when(jnp.logical_not(here))
                def _(copy=copy):
                    copy.start()

    def body(s, _):
        slot = s // 4 + 1

        @pl.when(s % 4 == 0)
        def _():
            @pl.when(s < STEPS)
            def _():
                plane_done(s // 4)

        @pl.when(s % 4 == 1)
        def _():
            @pl.when(slot + 1 < LAYERS)
            def _():
                own_on(slot + 1)

            @pl.when(slot < LAYERS)
            def _():
                line_on(slot)

        @pl.when(s % 4 == 2)
        def _():
            @pl.when(slot + 2 < LAYERS)
            def _():
                own_out(slot + 2)

            @pl.when(slot + 1 < LAYERS)
            def _():
                line_out(slot + 1)

        @pl.when((s >= 4) & (s < STEPS))
        def _():
            last = s - 4
            chip_copy(last).wait_recv()
            pass_copy(last).start()
            y_copy(s % 4).wait_send()
            for copy in stat_copies(last):
                copy.wait()
            core_copy(last).wait()
            chip_copy(last).wait_send()
            pass_copy(last).wait()
            normalise(s)

        @pl.when(s < STEPS)
        def _():
            multiply(s)

        @pl.when(s >= 2)
        def _():
            receive(s - 2)

        return 0

    lax.fori_loop(0, STEPS + 2, body, 0)

    for k in range(CHUNKS):
        for part in (0, 1):
            final_recv(k, part).wait()
        y_copy(k).wait_send()
        for t, copy in enumerate(final_copies(k)):
            here = (zh == t) & (zl == b) & (c == a)

            @pl.when(jnp.logical_not(here))
            def _(copy=copy):
                copy.wait_send()

    token_copy().wait_send()
    meta_copy().wait_send()
    share_copy().wait_send()
    for l in range(LAYERS):
        for phase in (0, 1):
            for kind in (0, 1, 2):
                for copy in both(l, phase, kind):
                    copy.wait_send()
        keep, give, same, cross = weight_copies(l)

        @pl.when(c == a)
        def _():
            give.wait_send()

        @pl.when(c != a)
        def _():
            same.wait_send()
            cross.wait_send()

        for j, (src, dst) in enumerate(((pv, params_out), (mv, moments_out), (vv, seconds_out))):
            pltpu.make_async_copy(src.at[l], dst.at[l], out_sem.at[l, j]).wait()


def per_device(
    tokens, counts, patch_index, clip_limit, norm_gain, params, moments, seconds, gradients
):
    any_space = pl.BlockSpec(memory_space=pl.ANY)
    vmem = pl.BlockSpec(memory_space=pltpu.VMEM)
    smem = pl.BlockSpec(memory_space=pltpu.SMEM)
    master = jax.ShapeDtypeStruct((LAYERS, ROWS, 1024), F32)
    dma = pltpu.SemaphoreType.DMA
    return pl.pallas_call(
        kernel,
        out_shape=(master, master, master, jax.ShapeDtypeStruct((512, 1024), BF)),
        in_specs=[any_space, smem, vmem, smem, vmem] + [any_space] * 4,
        out_specs=(any_space,) * 4,
        scratch_shapes=[
            pltpu.VMEM((LAYERS, ROWS, 1024), F32),
            pltpu.VMEM((LAYERS, ROWS, 1024), F32),
            pltpu.VMEM((LAYERS, ROWS, 1024), F32),
            pltpu.VMEM((LAYERS, ROWS, 1024), F32),
            pltpu.VMEM((LAYERS, 2, ROWS, HALF), BF),
            pltpu.VMEM((LAYERS, 2, 4, 4, ROWS, HALF), BF),
            pltpu.VMEM((4, 512, 1024), BF),
            pltpu.VMEM((2, 512, 1024), BF),
            pltpu.VMEM((2, CHUNKS, 4, 2, ROWS, HALF), BF),
            pltpu.VMEM((CHUNKS, 2, ROWS, HALF), F32),
            pltpu.VMEM((CHUNKS, 2, ROWS, HALF), BF),
            pltpu.VMEM((CHUNKS, 2, ROWS, HALF), BF),
            pltpu.VMEM((2, 2 * ROWS, HALF), F32),
            pltpu.VMEM((4, ROWS, 1024), F32),
            pltpu.VMEM((STEPS - 4, 8, 8, 2 * ROWS), F32),
            pltpu.VMEM((CHUNKS, 2, ROWS, HALF), BF),
            pltpu.VMEM((128, 2048), BF),
            pltpu.VMEM((CHUNKS, 2, ROWS, 1), F32),
            pltpu.VMEM((CHUNKS, 8, 128), F32),
            pltpu.VMEM((CHUNKS, 8, 128), F32),
            pltpu.VMEM((3, 8, 8, 128), F32),
            dma((LAYERS, 4)),
            dma((LAYERS, 3)),
            dma((4,)),
            dma((3, 7)),
            dma((3, 7)),
            dma((LAYERS, 2)),
            dma((LAYERS, 2)),
            dma((LAYERS, 24)),
            dma((LAYERS, 24)),
            dma((3,)),
            dma((3,)),
            dma((4,)),
            dma((4,)),
            dma((8,)),
            dma((8,)),
            dma((8,)),
            dma((8,)),
            dma((8,)),
            dma((8,)),
            dma((8, 8)),
            dma((8, 8)),
            dma((CHUNKS, 2)),
            dma((CHUNKS, 2)),
        ],
        compiler_params=pltpu.CompilerParams(
            collective_id=0, has_side_effects=True, vmem_limit_bytes=64 * 1024 * 1024 - 65536
        ),
    )(
        tokens,
        counts.reshape(1, 1),
        patch_index.reshape(512, 1),
        clip_limit.reshape(1, 1),
        norm_gain.reshape(32, HALF),
        params,
        moments,
        seconds,
        gradients,
    )


def solution(mesh):
    shard = P(None, "dp", "fsdp")
    return jax.shard_map(
        per_device,
        mesh=mesh,
        in_specs=(P("dp", None), P("dp"), P("dp"), P(), P(), shard, shard, shard, shard),
        out_specs=(shard, shard, shard, P("dp", "fsdp")),
        check_vma=False,
    )
```

time: 537 us -> 203 us (0.38)
  waiting for transfers between devices: 377 us -> 0 us
  Pallas kernels: 0 us -> 187 us
  other arithmetic: 60.2 us -> 0 us
  blocking collectives: 39.6 us -> 0 us
  matrix products: 38.4 us -> 0 us
  between operations: 16.1 us -> 1.94 us
  local copies, waits for them, and re-layouts: 4.64 us -> 11.6 us
    all_gather x4 -> x0, waiting for transfers between devices: 377 us -> none  [the longest x1 236 us: per_device(): gathered = lax.all_gather(weights, DP, axis=1, tiled=True)]
    pallas_call x0 -> x1, Pallas kernels: none -> 187 us  [per_device(): pl.pallas_call(kernel, out_shape=(master, master, master, jax.ShapeDtypeS...]
    psum x5 -> x0, blocking collectives: 39.6 us -> none  [one_axis_at_a_time(): x = lax.psum(x, axis)]
    dot_general x4 -> x0, matrix products: 38.4 us -> none  [per_device(): jnp.dot(normed, gathered[current], preferred_element_type=jnp.float32)]
    reduce_sum x9 -> x0, other arithmetic: 37.5 us -> none  [the longest x4 23.1 us: layer_norm(): centre = jnp.mean(stream, axis=1, keepdims=True)]
    sin x1 -> x0, other arithmetic: 14.7 us -> none  [position_code(): jnp.sin(across)]
    convert_element_type x2 -> x0, other arithmetic: 7.96 us -> none  [the longest x1 7.94 us: per_device(): weights = params_new.astype(jnp.bfloat16)]
  transfers between devices with their start and end apart: 4 -> 0, of which waited for: 4 -> 0; matrix products, arithmetic and copies ran while one was open for 3% -> 0% of each run, Pallas kernels for 0% -> 0%
where the time goes in v1:
time: 203 us; the launch traced here: 201 us
  Pallas kernels  187 us (92%)
  local copies, waits for them, and re-layouts  11.6 us (6%)
    pallas_call x1, Pallas kernels, per_device(): pl.pallas_call(kernel, out_shape=(master, master, master, jax.ShapeDtypeS...  187 us
    unnamed x10, local copies, waits for them, and re-layouts  8.59 us

profile of v1, /device:TPU:1, one launch (start us, length us, event | category | flops | bytes accessed | tf_op | source)
XLA Modules:
  0.0 201.0 jit_solution(9840776850174876397)
XLA Ops:
  1.9 1.5 reshape.23.gain_ref
  3.4 1.5 copy.13.patch_ref
  5.0 187.4 %shard_map.120 = (f32[4,128,1024]{2,1,0:T(8,128)}, f32[4,128,1024]{2,1,0:T(8,128)}, f32[4,128,1024]{2,1,0:T(8,128)}, bf16[512,1024]{1,0:T(8,128)(2,1)}) custom-call(bf16[512,4096]{1,0:T(8,128)(2,1)} %tokens_hbm.1, s32[1,1]{1,0:T(1,128)} %bitcast.3.counts_ref, s32[512,1]{1,0:T(8,128)} %copy.13.patch_ref, f32[1,1]{1,0:T(1,128)} %bitcast.4.clip_ref, ...), custom_call_target="tpu_custom_call" | custom-call | tf_op jit(solution)/shard_map/pallas_call | solution.py:557
  192.4 0.0 copy-start.1
  192.4 3.3 %copy.20 = f32[4,128,1024]{2,1,0:T(8,128)} copy(f32[4,128,1024]{2,1,0:T(8,128)} %get-tuple-element.8) | data formatting | bytes 4194304
  195.7 0.0 copy-done.1
  195.7 0.0 copy-start
  195.7 1.3 copy.21
  197.0 1.0 copy-done
  198.1 0.0 copy-start.2
  198.1 1.3 copy.22
  199.4 0.6 copy-done.2
  200.0 1.0 copy.23
Async XLA Ops:
  192.4 3.3 %copy-start.1 = (f32[4,128,1024]{2,1,0:T(8,128)S(1)}, f32[4,128,1024]{2,1,0:T(8,128)}, u32[]{:S(2)}) copy-start(f32[4,128,1024]{2,1,0:T(8,128)} %get-tuple-element.9) | copy-start | bytes 6291460
  195.7 2.3 %copy-start = (f32[4,128,1024]{2,1,0:T(8,128)S(1)}, f32[4,128,1024]{2,1,0:T(8,128)}, u32[]{:S(2)}) copy-start(f32[4,128,1024]{2,1,0:T(8,128)} %get-tuple-element.10) | copy-start | bytes 6291460
  198.1 2.0 copy-start.2

commit v2 on v1

v2 whole, which is shorter than its diff:
```python
import functools
import math

import jax
import jax.numpy as jnp
from jax import lax
from jax.experimental import pallas as pl
from jax.experimental.pallas import tpu as pltpu
from jax.sharding import PartitionSpec as P

D = 4096
LAYERS = 4
STEP = 40
ROWS = 128
HALF = 512
CHUNKS = 4
STEPS = LAYERS * CHUNKS

beta_one = 0.9
beta_two = 0.95
adam_eps = 1e-08
learning_rate = 0.0024
weight_decay = 0.05
norm_eps = 1e-06
BF = jnp.bfloat16
F32 = jnp.float32
MESH = pl.DeviceIdType.MESH


def kernel(
    tokens_hbm, counts_ref, patch_hbm, clip_ref, gain_hbm, params_hbm, moments_hbm, seconds_hbm,
    gradients_hbm, params_out, moments_out, seconds_out, mixed_out,
    pv, mv, vv, gv, wb, tok, oth, xbuf, stream, ysend, yrecv, acc, statbuf,
    table, valid, meta_s, meta_r, red, patch_ref, gain_raw, gain_ref,
    in_sem, out_sem, tok_sem, small_sem, red_s, red_r, wx_s, wx_r, ag_s, ag_r, ts_s, ts_r,
    y_s, y_r, yl_s, yl_r, xd_s, xd_r, xi_s, xi_r, f_s, f_r, st_s, st_r, fin_s, fin_r,
):
    dp = lax.axis_index("dp")
    fs = lax.axis_index("fsdp")
    x = dp % 4
    y = (dp // 4) % 4
    zh = dp // 16
    zl = fs // 2
    c = fs % 2
    b = zh
    a = (zl + zh) % 2
    mine = 2 * a + c

    def flip(v, bit):
        return 1 - v if bit else v

    def at(xx, yy, hh, ll, cc):
        return (hh * 16 + yy * 4 + xx, ll * 2 + cc)

    def along_x(d):
        return at((x + d) % 4, y, zh, zl, c)

    def along_y(d):
        return at(x, (y + d) % 4, zh, zl, c)

    def column(r):
        return at(x, y, flip(zh, r & 4), flip(zl, r & 2), flip(c, r & 1))

    def block_of(r):
        return 2 * flip(a, r & 2) + flip(c, r & 1)

    core_peer = column(1)
    x_peer = column(2)
    y_peer = column(6)

    def remote(src, dst, ssem, rsem, dev):
        return pltpu.make_async_remote_copy(
            src_ref=src, dst_ref=dst, send_sem=ssem, recv_sem=rsem, device_id=dev,
            device_id_type=MESH,
        )

    for l in range(LAYERS):
        for h in range(2):
            pltpu.make_async_copy(
                gradients_hbm.at[l, :, pl.ds(HALF * h, HALF)], gv.at[l, h], in_sem.at[l, 1]
            ).start()
    barrier = pltpu.get_barrier_semaphore()
    plane = [
        at((x + i) % 4, (y + j) % 4, zh, zl, c) for j in range(4) for i in range(4) if i or j
    ]
    others = plane + [column(r) for r in range(1, 8)]
    for dev in others:
        pl.semaphore_signal(barrier, inc=1, device_id=dev, device_id_type=MESH)
    for l in range(LAYERS):
        for src, dst in ((params_hbm, pv), (moments_hbm, mv), (seconds_hbm, vv)):
            pltpu.make_async_copy(src.at[l], dst.at[l], in_sem.at[l, 0]).start()
    for q in range(4):
        pltpu.make_async_copy(
            tokens_hbm.at[:, pl.ds(1024 * q, 1024)], tok.at[q], tok_sem.at[0]
        ).start()
    small = [pltpu.make_async_copy(gain_hbm, gain_raw, small_sem.at[0])]
    for k in range(CHUNKS):
        small.append(
            pltpu.make_async_copy(
                patch_hbm.at[pl.ds(ROWS * k, ROWS)], patch_ref.at[k], small_sem.at[1]
            )
        )
    for copy in small:
        copy.start()

    total = jnp.zeros((8, HALF), F32)
    for l in range(LAYERS):
        pltpu.make_async_copy(gv.at[l], gv.at[l], in_sem.at[l, 1]).wait()

        def squares(i, part, l=l):
            for h in range(2):
                g = gv[l, h, pl.ds(pl.multiple_of(i * 32, 32), 32), :]
                g = g * g
                part = part + ((g[0:8] + g[8:16]) + (g[16:24] + g[24:32]))
            return part

        total = lax.fori_loop(0, 4, squares, total)
    tile = total[:, 0:128]
    for i in range(1, 4):
        tile = tile + total[:, 128 * i : 128 * (i + 1)]
    with jax.named_scope("barrier"):
        pl.semaphore_wait(barrier, len(others))

    def exchange(stage, devs, tile, filler):
        red[stage, 0] = tile
        copies = [
            remote(
                red.at[stage, 0], red.at[stage, r + 1], red_s.at[stage], red_r.at[stage], dev
            )
            for r, dev in enumerate(devs)
        ]
        for copy in copies:
            copy.start()
        filler()
        with jax.named_scope("reduce_wait"):
            came = red.at[stage, pl.ds(1, len(devs))]
            pltpu.make_async_copy(came, came, red_s.at[stage]).wait()
            pltpu.make_async_copy(came, came, red_r.at[stage]).wait()
            for r in range(len(devs)):
                tile = tile + red[stage, r + 1]
        return tile

    def token_copy(i):
        rows = pl.ds(256 * i, 256)
        return remote(
            tok.at[2 * (1 - b) + c, rows], oth.at[c, rows], ts_s.at[i], ts_r.at[i], y_peer
        )

    def fill_column():
        pltpu.make_async_copy(tok, tok, tok_sem.at[0]).wait()
        token_copy(0).start()
        token_copy(1).start()

    def fill_table():
        lane = lax.broadcasted_iota(jnp.int32, (16, 1024), 1).astype(F32)
        row = lax.broadcasted_iota(jnp.int32, (16, 1024), 0).astype(F32)
        angle = row * jnp.exp(lane * (-math.log(10000.0) / 1024.0))
        for q, wave in ((0, jnp.sin(angle)), (1, jnp.cos(angle))):
            cols = slice(1024 * q, 1024 * (q + 1))
            for i in range(3):
                piece = wave.astype(BF)
                table[16 * i : 16 * (i + 1), cols] = piece
                wave = wave - piece.astype(F32)
        table[48:128, :] = jnp.zeros((80, 2048), BF)
        small[0].wait()
        pltpu.make_async_copy(patch_ref, patch_ref, small_sem.at[1]).wait()
        for l in range(LAYERS):
            for i in range(8):
                gain_ref[8 * l + i : 8 * l + i + 1, :] = gain_raw[
                    l : l + 1, HALF * i : HALF * (i + 1)
                ]

    tile = exchange(0, [column(r) for r in range(1, 8)], tile, fill_column)
    tile = exchange(1, plane, tile, fill_table)
    norm = jnp.sqrt(jnp.sum(jnp.sum(tile, axis=1, keepdims=True), axis=0, keepdims=True))
    factor = jnp.minimum(1.0, clip_ref[0, 0] / (norm + 1e-06))

    def weight_copies(l):
        here = wb.at[l, zl, y, x]
        keep = pltpu.make_async_copy(ysend.at[l, c], here, wx_s.at[l, 1])
        give = remote(ysend.at[l, 1 - c], here, wx_s.at[l, 0], wx_r.at[l, 0], core_peer)
        same = remote(ysend.at[l, c], here, wx_s.at[l, 0], wx_r.at[l, 1], x_peer)
        cross = remote(ysend.at[l, 1 - c], here, wx_s.at[l, 1], wx_r.at[l, 1], column(3))
        return keep, give, same, cross

    for l in range(LAYERS):
        three = pv.at[pl.ds(0, 3)]
        pltpu.make_async_copy(three, three, in_sem.at[l, 0]).wait()

        def update(i, _, l=l):
            rows = pl.ds(pl.multiple_of(i * 16, 16), 16)
            p = pv[l, rows, :]
            clipped = jnp.concatenate([gv[l, 0, rows, :], gv[l, 1, rows, :]], axis=1) * factor
            m = beta_one * mv[l, rows, :] + (1.0 - beta_one) * clipped
            v = beta_two * vv[l, rows, :] + (1.0 - beta_two) * clipped * clipped
            root = jnp.sqrt(v * (1.0 / (1.0 - beta_two**STEP))) + adam_eps
            direction = (m * (1.0 / (1.0 - beta_one**STEP))) / root
            p = p - learning_rate * (direction + weight_decay * p)
            mv[l, rows, :] = m
            vv[l, rows, :] = v
            pv[l, rows, :] = p
            w = p.astype(BF)
            ysend[l, 0, rows, :] = w[:, 0:HALF]
            ysend[l, 1, rows, :] = w[:, HALF:]
            return 0

        with jax.named_scope("update"):
            lax.fori_loop(0, ROWS // 16, update, 0)
        own, give_core, same, cross = weight_copies(l)

        @pl.when(c == a)
        def _():
            own.start()
            give_core.start()

        @pl.when(c != a)
        def _():
            same.start()
            cross.start()

    def weights_kept():
        for l in range(LAYERS):

            @pl.when(c == a)
            def _(l=l):
                weight_copies(l)[0].wait()

    def weights_sent():
        for l in range(LAYERS):
            keep, give_core, same, cross = weight_copies(l)

            @pl.when(c == a)
            def _():
                give_core.wait_send()

            @pl.when(c != a)
            def _():
                same.wait_send()
                cross.wait_send()

    def start_outputs():
        for l in range(LAYERS):
            for j, (src, dst) in enumerate(((pv, params_out), (mv, moments_out), (vv, seconds_out))):
                pltpu.make_async_copy(src.at[l], dst.at[l], out_sem.at[j]).start()

    def piece(q, h, phase, xx, yy, part):
        l, nb = q // 2, (1 - b) + (q % 2) * (2 * b - 1)
        if phase == 0:
            return wb.at[l, nb, yy, xx, pl.ds(64 * h + 32 * part, 32), :]
        if h == 0:
            return wb.at[l, nb, yy, pl.ds(2 * part, 2), pl.ds(0, 64), :]
        return wb.at[l, nb, pl.ds(2 * part, 2), xx, pl.ds(64, 64), :]

    def gather_copy(q, h, phase, sign, kind):
        on_x = (h == 0) == (phase == 0)
        step = 1 if sign == 0 else 3
        part = sign if kind != 1 else 1 - sign
        xx, yy = x, y
        if kind == 2:
            if on_x:
                xx = (x + 4 - step) % 4
            else:
                yy = (y + 4 - step) % 4
        ref = piece(q, h, phase, xx, yy, part)
        group = 2 * phase + (0 if kind == 0 else 1)
        out = (2 * phase + 1) if kind == 2 else 2 * phase
        dev = along_x(step) if on_x else along_y(step)
        return remote(ref, ref, ag_s.at[q, out], ag_r.at[q, group], dev)

    def both(q, phase, kind):
        return [gather_copy(q, h, phase, sign, kind) for h in (0, 1) for sign in (0, 1)]

    def start_all(copies):
        for copy in copies:
            copy.start()

    def group_ref(q, group):
        l, nb = q // 2, q % 2
        if group < 2:
            return wb.at[l, nb, 0, pl.ds(0, group + 1)]
        return wb.at[l, nb, pl.ds(0, group - 1)]

    def recv_group(q, group):
        ref = group_ref(q, group)
        pltpu.make_async_copy(ref, ref, ag_r.at[q, group]).wait()

    def sent_group(q, group):
        ref = group_ref(q, group ^ 1)
        pltpu.make_async_copy(ref, ref, ag_s.at[q, group]).wait()

    def own_out(q):
        with jax.named_scope("own_out"):
            l, nb = q // 2, (1 - b) + (q % 2) * (2 * b - 1)
            here = wb.at[l, nb, y, x]

            @pl.when((c != a) | (nb != zl))
            def _():
                pltpu.make_async_copy(here, here, wx_r.at[l, (nb + zl) % 2]).wait()

            start_all(both(q, 0, 0))
            start_all(both(q, 0, 1))

    def own_on(q):
        with jax.named_scope("own_on"):
            recv_group(q, 0)
            start_all(both(q, 0, 2))

    def line_out(q):
        with jax.named_scope("line_out"):
            recv_group(q, 1)
            start_all(both(q, 1, 0))
            start_all(both(q, 1, 1))

    def line_on(q):
        with jax.named_scope("line_on"):
            recv_group(q, 2)
            start_all(both(q, 1, 2))

    def plane_done(q):
        with jax.named_scope("plane_done"):
            recv_group(q, 3)

    lane = lax.broadcasted_iota(jnp.int32, (ROWS, 128), 1)
    lane_f = lane.astype(F32)

    def spread(index):
        hit = (lane_f == index) | (lane_f == index + 16.0) | (lane_f == index + 32.0)
        return jnp.where(hit, 1.0, 0.0).astype(BF)

    def code(index, q):
        return jnp.dot(
            spread(index), table[:, 1024 * q : 1024 * (q + 1)], preferred_element_type=F32
        )

    def place(k, side, blocks, centre, scale):
        for q in range(2):
            for h in range(2):
                i = 2 * q + h
                values = blocks[i]
                gain = gain_ref[pl.ds(4 * b + i, 1), :]
                xbuf[0, k, i, side] = ((values - centre) * scale * gain).astype(BF)

                @pl.when(mine == i)
                def _(values=values):
                    stream[k, side] = values

    def embed_own(k):
        with jax.named_scope("embed_own"):
            rows = slice(ROWS * k, ROWS * (k + 1))
            p = jnp.broadcast_to(patch_ref[k : k + 1, :], (ROWS, 128)).T[:, 0:1]
            high = (p // 16).astype(F32)
            low = (p % 16).astype(F32)
            slot = lax.broadcasted_iota(jnp.int32, (ROWS, 1), 0) + ROWS * k
            real = jnp.where(slot < counts_ref[0], 1.0, 0.0)
            centre = jnp.zeros((ROWS, 1), F32)
            for q in range(4):
                values = tok[q, rows, :].astype(F32) + code(high if q < 2 else low, q % 2)
                values = jnp.where(real > 0.5, values, 0.0)
                gv[q, 0] = values[:, 0:HALF]
                gv[q, 1] = values[:, HALF:]
                centre = centre + jnp.sum(values, axis=1, keepdims=True)
            centre = centre * (1.0 / D)
            square = jnp.zeros((ROWS, 1), F32)
            for q in range(4):
                for h in range(2):
                    shifted = gv[q, h] - centre
                    square = square + jnp.sum(shifted * shifted, axis=1, keepdims=True)
            scale = lax.rsqrt(square * (1.0 / D) + norm_eps)
            place(k, zh, [gv[2 * b + i // 2, i % 2] for i in range(4)], centre, scale)
            valid[k, zh] = real
            cols = jnp.zeros((ROWS, 128), F32)
            for i, value in enumerate((centre, scale, high, low, real)):
                cols = jnp.where(lane == i, value, cols)
            meta_s[k] = cols.T[0:8, :]

    def meta_copy():
        return remote(meta_s, meta_r, ts_s.at[2], ts_r.at[2], y_peer)

    def share_copy(i):
        ref = oth.at[c, pl.ds(256 * i, 256)]
        return remote(ref, ref, ts_s.at[3 + i], ts_r.at[3 + i], core_peer)

    def embed_other(k):
        with jax.named_scope("embed_other"):
            rows = slice(ROWS * k, ROWS * (k + 1))
            cols = jnp.concatenate([meta_r[k]] * 16, axis=0).T
            centre, scale, high, low, real = [cols[:, i : i + 1] for i in range(5)]
            index = jnp.where(b == 0, high, low)
            blocks = []
            for q in range(2):
                values = oth[q, rows, :].astype(F32) + code(index, q)
                values = jnp.where(real > 0.5, values, 0.0)
                blocks += [values[:, 0:HALF], values[:, HALF:]]
            place(k, 1 - zh, blocks, centre, scale)
            valid[k, 1 - zh] = real

    def share(i):
        with jax.named_scope("token_wait"):
            token_copy(i).wait_recv()
        share_copy(i).start()

    def share(i):
        with jax.named_scope("token_wait"):
            token_copy(i).wait_recv()
        share_copy(i).start()

    def y_copy(k):
        return remote(ysend.at[k], yrecv.at[k], y_s.at[k], y_r.at[k], y_peer)

    def core_copy(s):
        ref = xbuf.at[(s // 4 + 1) % 2, s % 4, mine]
        return remote(ref, ref, xd_s.at[s % 8], xd_r.at[s % 8], core_peer)

    def chip_copy(s):
        ref = xbuf.at[(s // 4 + 1) % 2, s % 4, mine]
        return remote(ref, ref, xi_s.at[s % 8], xi_r.at[s % 8], x_peer)

    def pass_copy(s):
        ref = xbuf.at[(s // 4 + 1) % 2, s % 4, block_of(2)]
        return remote(ref, ref, f_s.at[s % 8], f_r.at[s % 8], core_peer)

    def stat_copies(s):
        return [
            remote(
                statbuf.at[s, 0], statbuf.at[s, r], st_s.at[s % 8], st_r.at[s % 8], column(r)
            )
            for r in range(1, 8)
        ]

    def final_place(k):
        return mixed_out.at[pl.ds(k * ROWS, ROWS), pl.ds(pl.multiple_of(c * HALF, HALF), HALF)]

    def final_copy(k):
        return remote(
            xbuf.at[0, k, 0, a], final_place(k), fin_s.at[k, 0], fin_r.at[k, c],
            at(x, y, zh, 1 - zl, a),
        )

    def final_core(k):
        return remote(
            xbuf.at[0, k, 0, 1 - a], final_place(k), fin_s.at[k, 1], fin_r.at[k, c], core_peer
        )

    def final_recv(k, part):
        dst = mixed_out.at[pl.ds(k * ROWS, ROWS), pl.ds(part * HALF, HALF)]
        return pltpu.make_async_copy(xbuf.at[0, k, 0, 0], dst, fin_r.at[k, part])

    def normalise(s):
        with jax.named_scope("normalise"):
            last = s - 4
            l, k = s // 4, s % 4
            means = [statbuf[last, r, 0:1, :] for r in range(8)]
            mean = means[0]
            for r in range(1, 8):
                mean = mean + means[r]
            mean = mean * 0.125
            spread_sum = jnp.zeros_like(mean)
            for r in range(8):
                off = means[r] - mean
                spread_sum = spread_sum + (statbuf[last, r, 1:2, :] + float(HALF) * off * off)
            scale = lax.rsqrt(spread_sum * (1.0 / D) + norm_eps)
            rows = jnp.concatenate([means[r] - mean for r in range(4)] + [scale] * 4, axis=0)
            cols = jnp.concatenate([rows] * 16, axis=0).T
            scale = cols[:, 4:5]
            for r in range(4):
                i = block_of(r)
                off = cols[:, r : r + 1]
                gain = gain_ref[pl.ds(8 * l + 4 * b + i, 1), :]
                d = xbuf[l % 2, k, i].reshape(2 * ROWS, HALF).astype(F32)
                xbuf[l % 2, k, i] = ((d + off) * scale * gain).astype(BF).reshape(2, ROWS, HALF)

    def product(s, h):
        l, k = s // 4, s % 4
        with jax.named_scope("product"):
            left = jnp.concatenate(
                [xbuf[l % 2, k, i].reshape(2 * ROWS, HALF) for i in range(4)], axis=1
            )

            def column_tile(n, _):
                cols = pl.ds(pl.multiple_of(n * 256, 256), 256)
                right = wb[l, h, :, :, :, cols].reshape(2048, 256)
                tile = jnp.dot(left, right, preferred_element_type=F32)
                acc[:, :, cols] = tile.reshape(2, ROWS, 256)
                return 0

            lax.fori_loop(0, 2, column_tile, 0)

    def last_copy(k, i):
        return remote(ysend.at[k, i], yrecv.at[k, i], yl_s.at[k, i], yl_r.at[k, i], y_peer)

    def give(s):
        k = s % 4
        product(s, 1 - b)

        @pl.when(s < STEPS - 4)
        def _():
            ysend[k] = acc[...].astype(BF)
            y_copy(k).start()

        @pl.when(s >= STEPS - 4)
        def _():
            ysend[k, 0] = acc[1 - b].astype(BF)
            last_copy(k, 0).start()
            gv[k, 0] = acc[b]

    def receive(s):
        k = s % 4
        product(s, b)
        with jax.named_scope("y_wait"):
            y_copy(k).wait_recv()
        with jax.named_scope("receive"):
            values = (stream[k] + acc[...] + yrecv[k].astype(F32)).reshape(2 * ROWS, HALF)
            stream[k] = values.reshape(2, ROWS, HALF)
            mean = jnp.sum(values, axis=1, keepdims=True) * (1.0 / HALF)
            d = values - mean
            square = jnp.sum(d * d, axis=1, keepdims=True)
            lanes = lax.broadcasted_iota(jnp.int32, (2 * ROWS, 128), 1)
            cols = jnp.where(lanes == 0, mean, jnp.where(lanes == 1, square, 0.0))
            statbuf[s, 0] = cols.T[0:2, :]
            xbuf[(s // 4 + 1) % 2, k, mine] = d.astype(BF).reshape(2, ROWS, HALF)
            start_all(stat_copies(s))
            chip_copy(s).start()
            core_copy(s).start()

    def give_rest(s):
        k = s % 4
        product(s, b)
        ysend[k, 1] = (acc[1 - b] + stream[k, 1 - b]).astype(BF)
        last_copy(k, 1).start()
        gv[k, 1] = acc[b] + stream[k, b]

    def finish(s, i):
        k = s % 4
        with jax.named_scope("y_wait"):
            last_copy(k, 1 - i).wait_recv()
        with jax.named_scope("finish"):
            real = valid[k, zh] > 0.5
            values = gv[k, i] + yrecv[k, 1 - i].astype(F32)
            xbuf[0, k, 0, i] = jnp.where(real, values, 0.0).astype(BF)

    def finish_both(s):
        k = s % 4
        finish(s, a)
        final_copy(k).start()
        finish(s, 1 - a)

        @pl.when(c == a)
        def _():
            dst = final_place(k)
            pltpu.make_async_copy(xbuf.at[0, k, 0, 1 - a], dst, fin_r.at[k, c]).start()

        @pl.when(c != a)
        def _():
            final_core(k).start()

    def body(s, _):
        @pl.when((s >= 4) & (s < STEPS))
        def _():
            with jax.named_scope("chip_wait"):
                chip_copy(s - 4).wait_recv()
            pass_copy(s - 4).start()

        @pl.when(s < STEPS - 2)
        def _():
            @pl.when(s % 4 == 2)
            def _():
                plane_done((s - 2) // 2 + 1)

            receive(s - 2)

        @pl.when((s == STEPS - 3) | (s == STEPS - 2))
        def _():
            @pl.when(s == STEPS - 3)
            def _():
                plane_done(2 * LAYERS - 1)

            give_rest(s - 1)

        @pl.when(s >= STEPS - 1)
        def _():
            finish_both(s - 3)

        @pl.when((s >= 4) & (s < STEPS))
        def _():
            last = s - 4
            with jax.named_scope("stat_wait"):
                y_copy(s % 4).wait_send()
                seven = statbuf.at[last, pl.ds(1, 7)]
                pltpu.make_async_copy(seven, seven, st_s.at[last % 8]).wait()
                pltpu.make_async_copy(seven, seven, st_r.at[last % 8]).wait()
            with jax.named_scope("block_wait"):
                core_copy(last).wait()
                chip_copy(last).wait_send()
                pass_copy(last).wait()
            normalise(s)

            @pl.when(s % 4 == 0)
            def _():
                plane_done(s // 2)

            late = s >= STEPS - 2

            @pl.when(late & (a == 0))
            def _():
                give_rest(s)

            give(s)

            @pl.when(late & (a == 1))
            def _():
                give_rest(s)

        @pl.when((s % 2 == 0) & (s < STEPS - 2))
        def _():
            line_on(s // 2 + 1)

        @pl.when((s % 2 == 1) & (s < STEPS - 3))
        def _():
            q = (s + 1) // 2
            line_out(q + 1)

            @pl.when(q + 2 < 2 * LAYERS)
            def _():
                own_on(q + 2)

            @pl.when(q + 3 < 2 * LAYERS)
            def _():
                own_out(q + 3)

        return 0

    weights_kept()
    own_out(0)
    embed_own(0)
    own_on(0)
    own_out(1)
    embed_own(1)
    line_out(0)
    embed_own(2)
    embed_own(3)
    meta_copy().start()
    start_outputs()
    line_on(0)
    own_on(1)
    own_out(2)
    share(0)
    with jax.named_scope("meta_wait"):
        meta_copy().wait_recv()
        share_copy(0).wait_recv()
    embed_other(0)
    share(1)
    plane_done(0)
    weights_sent()
    give(0)
    line_out(1)
    own_on(2)
    own_out(3)
    embed_other(1)
    give(1)
    line_on(1)
    with jax.named_scope("share_wait"):
        share_copy(1).wait_recv()
    embed_other(2)
    give(2)
    embed_other(3)
    give(3)
    line_out(2)
    own_on(3)
    own_out(4)
    lax.fori_loop(2, STEPS + 3, body, 0)

    for k in range(CHUNKS):
        with jax.named_scope("final_wait"):
            for part in (0, 1):
                final_recv(k, part).wait()
        for i in range(2):
            last_copy(k, i).wait_send()
        final_copy(k).wait_send()

        @pl.when(c != a)
        def _(k=k):
            final_core(k).wait_send()

    with jax.named_scope("end_wait"):
        meta_copy().wait_send()
    for i in range(2):
        token_copy(i).wait_send()
        share_copy(i).wait_send()
    def sent(q, _):
        for group in range(4):
            sent_group(q, group)
        return 0

    with jax.named_scope("end_sent"):
        lax.fori_loop(0, 2 * LAYERS, sent, 0)
    for j, dst in enumerate((pv, mv, vv)):
        pltpu.make_async_copy(dst, dst, out_sem.at[j]).wait()


def hand_over(p, m, v, mixed, p_out, m_out, v_out, mixed_out, sem):
    copies = [
        pltpu.make_async_copy(src, dst, sem.at[j])
        for j, (src, dst) in enumerate(((p, p_out), (m, m_out), (v, v_out), (mixed, mixed_out)))
    ]
    for copy in copies:
        copy.start()
    for copy in copies:
        copy.wait()


def per_device(
    tokens, counts, patch_index, clip_limit, norm_gain, params, moments, seconds, gradients
):
    any_space = pl.BlockSpec(memory_space=pl.ANY)
    hbm = pl.BlockSpec(memory_space=pltpu.HBM)
    smem = pl.BlockSpec(memory_space=pltpu.SMEM)
    master = jax.ShapeDtypeStruct((LAYERS, ROWS, 1024), F32)
    dma = pltpu.SemaphoreType.DMA
    shapes = (master, master, master, jax.ShapeDtypeStruct((512, 1024), BF))
    results = pl.pallas_call(
        kernel,
        out_shape=shapes,
        in_specs=[hbm, smem, hbm, smem, hbm] + [hbm] * 4,
        out_specs=(any_space,) * 4,
        scratch_shapes=[
            pltpu.VMEM((LAYERS, ROWS, 1024), F32),
            pltpu.VMEM((LAYERS, ROWS, 1024), F32),
            pltpu.VMEM((LAYERS, ROWS, 1024), F32),
            pltpu.VMEM((LAYERS, 2, ROWS, HALF), F32),
            pltpu.VMEM((LAYERS, 2, 4, 4, ROWS, HALF), BF),
            pltpu.VMEM((4, 512, 1024), BF),
            pltpu.VMEM((2, 512, 1024), BF),
            pltpu.VMEM((2, CHUNKS, 4, 2, ROWS, HALF), BF),
            pltpu.VMEM((CHUNKS, 2, ROWS, HALF), F32),
            pltpu.VMEM((CHUNKS, 2, ROWS, HALF), BF),
            pltpu.VMEM((CHUNKS, 2, ROWS, HALF), BF),
            pltpu.VMEM((2, ROWS, HALF), F32),
            pltpu.VMEM((STEPS - 4, 8, 2, 2 * ROWS), F32),
            pltpu.VMEM((128, 2048), BF),
            pltpu.VMEM((CHUNKS, 2, ROWS, 1), F32),
            pltpu.VMEM((CHUNKS, 8, 128), F32),
            pltpu.VMEM((CHUNKS, 8, 128), F32),
            pltpu.VMEM((2, 16, 8, 128), F32),
            pltpu.VMEM((CHUNKS, 128), jnp.int32),
            pltpu.VMEM((LAYERS, D), F32),
            pltpu.VMEM((32, HALF), F32),
            dma((LAYERS, 2)),
            dma((3,)),
            dma((1,)),
            dma((2,)),
            dma((2,)),
            dma((2,)),
            dma((LAYERS, 2)),
            dma((LAYERS, 2)),
            dma((2 * LAYERS, 4)),
            dma((2 * LAYERS, 4)),
            dma((5,)),
            dma((5,)),
            dma((4,)),
            dma((4,)),
            dma((CHUNKS, 2)),
            dma((CHUNKS, 2)),
            dma((8,)),
            dma((8,)),
            dma((8,)),
            dma((8,)),
            dma((8,)),
            dma((8,)),
            dma((8,)),
            dma((8,)),
            dma((CHUNKS, 2)),
            dma((CHUNKS, 2)),
        ],
        compiler_params=pltpu.CompilerParams(
            collective_id=0, has_side_effects=True, vmem_limit_bytes=49200000
        ),
    )(
        tokens,
        counts,
        pltpu.with_memory_space_constraint(patch_index, pltpu.HBM),
        clip_limit.reshape(1, 1),
        pltpu.with_memory_space_constraint(norm_gain, pltpu.HBM),
        params,
        moments,
        seconds,
        gradients,
    )
    return pl.pallas_call(
        hand_over,
        out_shape=shapes,
        in_specs=[any_space] * 4,
        out_specs=(any_space,) * 4,
        scratch_shapes=[
            dma((4,)),
        ],
        compiler_params=pltpu.CompilerParams(vmem_limit_bytes=1024 * 1024),
    )(*results)


def solution(mesh):
    shard = P(None, "dp", "fsdp")
    return jax.shard_map(
        per_device,
        mesh=mesh,
        in_specs=(P("dp", None), P("dp"), P("dp"), P(), P(), shard, shard, shard, shard),
        out_specs=(shard, shard, shard, P("dp", "fsdp")),
        check_vma=False,
    )
```

time: 203 us -> 149 us (0.73)
  Pallas kernels: 187 us -> 147 us
  local copies, waits for them, and re-layouts: 11.6 us -> 0 us
    pallas_call x1 -> x2, Pallas kernels: 187 us -> 147 us  [the longest x1 144 us: per_device(): pl.pallas_call(kernel, out_shape=shapes, in_specs=[hbm, smem, hbm, smem,...]
    unnamed x10 -> x0, local copies, waits for them, and re-layouts: 8.59 us -> none
    reshape x2 -> x0, local copies, waits for them, and re-layouts: 3.05 us -> none  [the longest x1 1.53 us: per_device(): patch_index.reshape(512, 1)]
where the time goes in v2:
time: 149 us
  Pallas kernels  147 us (99%)
  between operations  2.09 us (1%)
    pallas_call x1, Pallas kernels, per_device(): pl.pallas_call(kernel, out_shape=shapes, in_specs=[hbm, smem, hbm, smem,...  144 us
    pallas_call x1, Pallas kernels, per_device(): pl.pallas_call(hand_over, out_shape=shapes, in_specs=[any_space] * 4, out...  3.02 us

profile of v2, /device:TPU:1, one launch (start us, length us, event | category | flops | bytes accessed | tf_op | source)
XLA Modules:
  0.0 148.9 jit_solution(15654740895198715659)
XLA Ops:
  1.9 143.8 %shard_map.120 = (f32[4,128,1024]{2,1,0:T(8,128)S(1)}, f32[4,128,1024]{2,1,0:T(8,128)S(1)}, f32[4,128,1024]{2,1,0:T(8,128)S(1)}, bf16[512,1024]{1,0:T(8,128)(2,1)S(1)}) custom-call(bf16[512,4096]{1,0:T(8,128)(2,1)} %tokens_hbm.1, s32[1]{0:T(128)S(6)} %copy.13.counts_ref, s32[512]{0:T(512)} %patch_hbm.1, f32[1,1]{1,0:T(1,128)} %bitcast.1.clip_ref, ...), custom_call_target="tpu_custom_call" | custom-call | tf_op jit(solution)/shard_map/pallas_call | solution.py:720
  145.7 3.0 %shard_map.121 = (f32[4,128,1024]{2,1,0:T(8,128)}, f32[4,128,1024]{2,1,0:T(8,128)}, f32[4,128,1024]{2,1,0:T(8,128)}, bf16[512,1024]{1,0:T(8,128)(2,1)}) custom-call(f32[4,128,1024]{2,1,0:T(8,128)S(1)} %get-tuple-element.8.p, f32[4,128,1024]{2,1,0:T(8,128)S(1)} %get-tuple-element.9.m, f32[4,128,1024]{2,1,0:T(8,128)S(1)} %get-tuple-element.10.v, ...), custom_call_target="tpu_custom_call" | custom-call | tf_op jit(solution)/shard_map/pallas_call | solution.py:788

commit v3 on v2

--- a/solution.py
+++ b/solution.py
@@ -612,20 +612,21 @@
 
         @pl.when((s % 2 == 0) & (s < STEPS - 2))
         def _():
-            line_on(s // 2 + 1)
+            q = s // 2 + 1
+
+            @pl.when(q + 1 < 2 * LAYERS)
+            def _():
+                own_on(q + 1)
+
+            line_on(q)
+
+            @pl.when(q + 2 < 2 * LAYERS)
+            def _():
+                own_out(q + 2)
 
         @pl.when((s % 2 == 1) & (s < STEPS - 3))
         def _():
-            q = (s + 1) // 2
-            line_out(q + 1)
-
-            @pl.when(q + 2 < 2 * LAYERS)
-            def _():
-                own_on(q + 2)
-
-            @pl.when(q + 3 < 2 * LAYERS)
-            def _():
-                own_out(q + 3)
+            line_out((s + 3) // 2)
 
         return 0
 
@@ -637,37 +638,40 @@
     embed_own(1)
     line_out(0)
     embed_own(2)
+    own_on(1)
     embed_own(3)
     meta_copy().start()
     start_outputs()
     line_on(0)
-    own_on(1)
-    own_out(2)
     share(0)
     with jax.named_scope("meta_wait"):
         meta_copy().wait_recv()
         share_copy(0).wait_recv()
     embed_other(0)
+    own_out(2)
+    line_out(1)
     share(1)
     plane_done(0)
     weights_sent()
     give(0)
-    line_out(1)
     own_on(2)
-    own_out(3)
     embed_other(1)
     give(1)
     line_on(1)
+    own_out(3)
     with jax.named_scope("share_wait"):
         share_copy(1).wait_recv()
     embed_other(2)
     give(2)
     embed_other(3)
+    line_out(2)
+    plane_done(1)
+    receive(0)
     give(3)
-    line_out(2)
     own_on(3)
+    line_on(2)
     own_out(4)
-    lax.fori_loop(2, STEPS + 3, body, 0)
+    lax.fori_loop(3, STEPS + 3, body, 0)
 
     for k in range(CHUNKS):
         with jax.named_scope("final_wait"):

time: 149 us -> 147 us (0.987)
  Pallas kernels: 147 us -> 145 us
    pallas_call x1, Pallas kernels: 144 us -> 142 us  [per_device(): pl.pallas_call(kernel, out_shape=shapes, in_specs=[hbm, smem, hbm, smem,...]
where the time goes in v3:
time: 147 us
  Pallas kernels  145 us (99%)
  between operations  2.09 us (1%)
    pallas_call x1, Pallas kernels, per_device(): pl.pallas_call(kernel, out_shape=shapes, in_specs=[hbm, smem, hbm, smem,...  142 us
    pallas_call x1, Pallas kernels, per_device(): pl.pallas_call(hand_over, out_shape=shapes, in_specs=[any_space] * 4, out...  3.02 us

profile of v3, /device:TPU:1, one launch (start us, length us, event | category | flops | bytes accessed | tf_op | source)
XLA Modules:
  0.0 146.7 jit_solution(8522072734868213753)
XLA Ops:
  1.9 141.6 %shard_map.120 = (f32[4,128,1024]{2,1,0:T(8,128)S(1)}, f32[4,128,1024]{2,1,0:T(8,128)S(1)}, f32[4,128,1024]{2,1,0:T(8,128)S(1)}, bf16[512,1024]{1,0:T(8,128)(2,1)S(1)}) custom-call(bf16[512,4096]{1,0:T(8,128)(2,1)} %tokens_hbm.1, s32[1]{0:T(128)S(6)} %copy.13.counts_ref, s32[512]{0:T(512)} %patch_hbm.1, f32[1,1]{1,0:T(1,128)} %bitcast.1.clip_ref, ...), custom_call_target="tpu_custom_call" | custom-call | tf_op jit(solution)/shard_map/pallas_call | solution.py:724
  143.5 3.0 %shard_map.121 = (f32[4,128,1024]{2,1,0:T(8,128)}, f32[4,128,1024]{2,1,0:T(8,128)}, f32[4,128,1024]{2,1,0:T(8,128)}, bf16[512,1024]{1,0:T(8,128)(2,1)}) custom-call(f32[4,128,1024]{2,1,0:T(8,128)S(1)} %get-tuple-element.8.p, f32[4,128,1024]{2,1,0:T(8,128)S(1)} %get-tuple-element.9.m, f32[4,128,1024]{2,1,0:T(8,128)S(1)} %get-tuple-element.10.v, ...), custom_call_target="tpu_custom_call" | custom-call | tf_op jit(solution)/shard_map/pallas_call | solution.py:792

commit v4 on v3

--- a/solution.py
+++ b/solution.py
@@ -15,6 +15,7 @@
 HALF = 512
 CHUNKS = 4
 STEPS = LAYERS * CHUNKS
+FIRST = 2 * LAYERS
 
 beta_one = 0.9
 beta_two = 0.95
@@ -177,10 +178,10 @@
 
     def weight_copies(l):
         here = wb.at[l, zl, y, x]
-        keep = pltpu.make_async_copy(ysend.at[l, c], here, wx_s.at[l, 1])
-        give = remote(ysend.at[l, 1 - c], here, wx_s.at[l, 0], wx_r.at[l, 0], core_peer)
-        same = remote(ysend.at[l, c], here, wx_s.at[l, 0], wx_r.at[l, 1], x_peer)
-        cross = remote(ysend.at[l, 1 - c], here, wx_s.at[l, 1], wx_r.at[l, 1], column(3))
+        keep = pltpu.make_async_copy(ysend.at[l, c], here, wx_s.at[1])
+        give = remote(ysend.at[l, 1 - c], here, wx_s.at[0], wx_r.at[l, 0], core_peer)
+        same = remote(ysend.at[l, c], here, wx_s.at[0], wx_r.at[l, 1], x_peer)
+        cross = remote(ysend.at[l, 1 - c], here, wx_s.at[1], wx_r.at[l, 1], column(3))
         return keep, give, same, cross
 
     for l in range(LAYERS):
@@ -218,25 +219,21 @@
             same.start()
             cross.start()
 
+    def four_blocks(sem):
+        ref = ysend.at[pl.ds(0, 2)]
+        pltpu.make_async_copy(ref, ref, sem).wait()
+
     def weights_kept():
-        for l in range(LAYERS):
-
-            @pl.when(c == a)
-            def _(l=l):
-                weight_copies(l)[0].wait()
+        @pl.when(c == a)
+        def _():
+            four_blocks(wx_s.at[1])
 
     def weights_sent():
-        for l in range(LAYERS):
-            keep, give_core, same, cross = weight_copies(l)
-
-            @pl.when(c == a)
-            def _():
-                give_core.wait_send()
-
-            @pl.when(c != a)
-            def _():
-                same.wait_send()
-                cross.wait_send()
+        four_blocks(wx_s.at[0])
+
+        @pl.when(c != a)
+        def _():
+            four_blocks(wx_s.at[1])
 
     def start_outputs():
         for l in range(LAYERS):
@@ -244,6 +241,13 @@
                 pltpu.make_async_copy(src.at[l], dst.at[l], out_sem.at[j]).start()
 
     def piece(q, h, phase, xx, yy, part):
+        if isinstance(q, int) and q in (0, FIRST):
+            cols = pl.ds(256 * (q // FIRST), 256)
+            if phase == 0:
+                return wb.at[0, 1 - b, yy, xx, pl.ds(64 * h + 32 * part, 32), cols]
+            if h == 0:
+                return wb.at[0, 1 - b, yy, pl.ds(2 * part, 2), pl.ds(0, 64), cols]
+            return wb.at[0, 1 - b, pl.ds(2 * part, 2), xx, pl.ds(64, 64), cols]
         l, nb = q // 2, (1 - b) + (q % 2) * (2 * b - 1)
         if phase == 0:
             return wb.at[l, nb, yy, xx, pl.ds(64 * h + 32 * part, 32), :]
@@ -263,9 +267,10 @@
                 yy = (y + 4 - step) % 4
         ref = piece(q, h, phase, xx, yy, part)
         group = 2 * phase + (0 if kind == 0 else 1)
-        out = (2 * phase + 1) if kind == 2 else 2 * phase
+        layer = 0 if isinstance(q, int) and q == FIRST else q // 2
+        out = layer if phase == 1 else LAYERS
         dev = along_x(step) if on_x else along_y(step)
-        return remote(ref, ref, ag_s.at[q, out], ag_r.at[q, group], dev)
+        return remote(ref, ref, ag_s.at[out], ag_r.at[q, group], dev)
 
     def both(q, phase, kind):
         return [gather_copy(q, h, phase, sign, kind) for h in (0, 1) for sign in (0, 1)]
@@ -275,6 +280,10 @@
             copy.start()
 
     def group_ref(q, group):
+        if isinstance(q, int) and q in (0, FIRST):
+            if group == 0:
+                return wb.at[0, 0, 0, 0, pl.ds(0, 64)]
+            return wb.at[0, 0, 0, pl.ds(0, 2 ** (group - 1))]
         l, nb = q // 2, q % 2
         if group < 2:
             return wb.at[l, nb, 0, pl.ds(0, group + 1)]
@@ -284,18 +293,15 @@
         ref = group_ref(q, group)
         pltpu.make_async_copy(ref, ref, ag_r.at[q, group]).wait()
 
-    def sent_group(q, group):
-        ref = group_ref(q, group ^ 1)
-        pltpu.make_async_copy(ref, ref, ag_s.at[q, group]).wait()
-
     def own_out(q):
         with jax.named_scope("own_out"):
-            l, nb = q // 2, (1 - b) + (q % 2) * (2 * b - 1)
-            here = wb.at[l, nb, y, x]
-
-            @pl.when((c != a) | (nb != zl))
-            def _():
-                pltpu.make_async_copy(here, here, wx_r.at[l, (nb + zl) % 2]).wait()
+            if not (isinstance(q, int) and q == FIRST):
+                l, nb = q // 2, (1 - b) + (q % 2) * (2 * b - 1)
+                here = wb.at[l, nb, y, x]
+
+                @pl.when((c != a) | (nb != zl))
+                def _():
+                    pltpu.make_async_copy(here, here, wx_r.at[l, (nb + zl) % 2]).wait()
 
             start_all(both(q, 0, 0))
             start_all(both(q, 0, 1))
@@ -309,6 +315,8 @@
         with jax.named_scope("line_out"):
             recv_group(q, 1)
             start_all(both(q, 1, 0))
+            if isinstance(q, int) and q == FIRST:
+                return
             start_all(both(q, 1, 1))
 
     def line_on(q):
@@ -409,20 +417,20 @@
 
     def core_copy(s):
         ref = xbuf.at[(s // 4 + 1) % 2, s % 4, mine]
-        return remote(ref, ref, xd_s.at[s % 8], xd_r.at[s % 8], core_peer)
+        return remote(ref, ref, xd_s.at[s % 4], xd_r.at[s % 8], core_peer)
 
     def chip_copy(s):
         ref = xbuf.at[(s // 4 + 1) % 2, s % 4, mine]
-        return remote(ref, ref, xi_s.at[s % 8], xi_r.at[s % 8], x_peer)
+        return remote(ref, ref, xi_s.at[s % 4], xi_r.at[s % 8], x_peer)
 
     def pass_copy(s):
         ref = xbuf.at[(s // 4 + 1) % 2, s % 4, block_of(2)]
-        return remote(ref, ref, f_s.at[s % 8], f_r.at[s % 8], core_peer)
+        return remote(ref, ref, f_s.at[s % 4], f_r.at[s % 8], core_peer)
 
     def stat_copies(s):
         return [
             remote(
-                statbuf.at[s, 0], statbuf.at[s, r], st_s.at[s % 8], st_r.at[s % 8], column(r)
+                statbuf.at[s, 0], statbuf.at[s, r], st_s.at[s % 4], st_r.at[s % 8], column(r)
             )
             for r in range(1, 8)
         ]
@@ -432,18 +440,14 @@
 
     def final_copy(k):
         return remote(
-            xbuf.at[0, k, 0, a], final_place(k), fin_s.at[k, 0], fin_r.at[k, c],
+            xbuf.at[0, k, 0, a], final_place(k), fin_s.at[0], fin_r.at[0],
             at(x, y, zh, 1 - zl, a),
         )
 
     def final_core(k):
         return remote(
-            xbuf.at[0, k, 0, 1 - a], final_place(k), fin_s.at[k, 1], fin_r.at[k, c], core_peer
+            xbuf.at[0, k, 0, 1 - a], final_place(k), fin_s.at[1], fin_r.at[0], core_peer
         )
-
-    def final_recv(k, part):
-        dst = mixed_out.at[pl.ds(k * ROWS, ROWS), pl.ds(part * HALF, HALF)]
-        return pltpu.make_async_copy(xbuf.at[0, k, 0, 0], dst, fin_r.at[k, part])
 
     def normalise(s):
         with jax.named_scope("normalise"):
@@ -469,7 +473,7 @@
                 d = xbuf[l % 2, k, i].reshape(2 * ROWS, HALF).astype(F32)
                 xbuf[l % 2, k, i] = ((d + off) * scale * gain).astype(BF).reshape(2, ROWS, HALF)
 
-    def product(s, h):
+    def product(s, h, first=0, tiles=2):
         l, k = s // 4, s % 4
         with jax.named_scope("product"):
             left = jnp.concatenate(
@@ -483,7 +487,43 @@
                 acc[:, :, cols] = tile.reshape(2, ROWS, 256)
                 return 0
 
-            lax.fori_loop(0, 2, column_tile, 0)
+            lax.fori_loop(first, first + tiles, column_tile, 0)
+
+    def part_copy(k, i):
+        ref = yrecv.at[k, :, :, pl.ds(256 * i, 256)]
+        return remote(
+            ysend.at[k, :, :, pl.ds(256 * i, 256)], ref, yl_s.at[k, i], yl_r.at[k, i], y_peer
+        )
+
+    def give_first(k, i):
+        product(k, 1 - b, i, 1)
+        cols = slice(256 * i, 256 * (i + 1))
+        ysend[k, :, :, cols] = acc[:, :, cols].astype(BF)
+        part_copy(k, i).start()
+
+    def received(s):
+        k = s % 4
+
+        @pl.when(s < 4)
+        def _():
+            part_copy(k, 0).wait_recv()
+            part_copy(k, 1).wait_recv()
+
+        @pl.when(s >= 4)
+        def _():
+            y_copy(k).wait_recv()
+
+    def sent_before(s):
+        k = s % 4
+
+        @pl.when(s < 8)
+        def _():
+            part_copy(k, 0).wait_send()
+            part_copy(k, 1).wait_send()
+
+        @pl.when(s >= 8)
+        def _():
+            y_copy(k).wait_send()
 
     def last_copy(k, i):
         return remote(ysend.at[k, i], yrecv.at[k, i], yl_s.at[k, i], yl_r.at[k, i], y_peer)
@@ -507,7 +547,7 @@
         k = s % 4
         product(s, b)
         with jax.named_scope("y_wait"):
-            y_copy(k).wait_recv()
+            received(s)
         with jax.named_scope("receive"):
             values = (stream[k] + acc[...] + yrecv[k].astype(F32)).reshape(2 * ROWS, HALF)
             stream[k] = values.reshape(2, ROWS, HALF)
@@ -547,7 +587,7 @@
         @pl.when(c == a)
         def _():
             dst = final_place(k)
-            pltpu.make_async_copy(xbuf.at[0, k, 0, 1 - a], dst, fin_r.at[k, c]).start()
+            pltpu.make_async_copy(xbuf.at[0, k, 0, 1 - a], dst, fin_r.at[0]).start()
 
         @pl.when(c != a)
         def _():
@@ -584,9 +624,9 @@
         def _():
             last = s - 4
             with jax.named_scope("stat_wait"):
-                y_copy(s % 4).wait_send()
+                sent_before(s)
                 seven = statbuf.at[last, pl.ds(1, 7)]
-                pltpu.make_async_copy(seven, seven, st_s.at[last % 8]).wait()
+                pltpu.make_async_copy(seven, seven, st_s.at[last % 4]).wait()
                 pltpu.make_async_copy(seven, seven, st_r.at[last % 8]).wait()
             with jax.named_scope("block_wait"):
                 core_copy(last).wait()
@@ -632,71 +672,76 @@
 
     weights_kept()
     own_out(0)
+    own_out(FIRST)
     embed_own(0)
     own_on(0)
+    own_on(FIRST)
     own_out(1)
     embed_own(1)
     line_out(0)
+    line_out(FIRST)
     embed_own(2)
     own_on(1)
     embed_own(3)
     meta_copy().start()
     start_outputs()
     line_on(0)
+    start_all(both(FIRST, 1, 1))
     share(0)
     with jax.named_scope("meta_wait"):
         meta_copy().wait_recv()
         share_copy(0).wait_recv()
+    line_on(FIRST)
+    own_out(2)
     embed_other(0)
-    own_out(2)
+    weights_sent()
+    plane_done(0)
+    give_first(0, 0)
     line_out(1)
     share(1)
-    plane_done(0)
-    weights_sent()
-    give(0)
+    embed_other(1)
+    give_first(1, 0)
     own_on(2)
-    embed_other(1)
-    give(1)
+    plane_done(FIRST)
+    give_first(0, 1)
+    give_first(1, 1)
     line_on(1)
     own_out(3)
     with jax.named_scope("share_wait"):
         share_copy(1).wait_recv()
     embed_other(2)
-    give(2)
+    give_first(2, 0)
+    give_first(2, 1)
     embed_other(3)
     line_out(2)
     plane_done(1)
     receive(0)
-    give(3)
+    give_first(3, 0)
+    give_first(3, 1)
     own_on(3)
     line_on(2)
     own_out(4)
     lax.fori_loop(3, STEPS + 3, body, 0)
 
+    with jax.named_scope("final_wait"):
+        pltpu.make_async_copy(mixed_out, mixed_out, fin_r.at[0]).wait()
+    four_blocks(fin_s.at[0])
+
+    @pl.when(c != a)
+    def _():
+        four_blocks(fin_s.at[1])
+
     for k in range(CHUNKS):
-        with jax.named_scope("final_wait"):
-            for part in (0, 1):
-                final_recv(k, part).wait()
         for i in range(2):
             last_copy(k, i).wait_send()
-        final_copy(k).wait_send()
-
-        @pl.when(c != a)
-        def _(k=k):
-            final_core(k).wait_send()
-
     with jax.named_scope("end_wait"):
         meta_copy().wait_send()
     for i in range(2):
         token_copy(i).wait_send()
         share_copy(i).wait_send()
-    def sent(q, _):
-        for group in range(4):
-            sent_group(q, group)
-        return 0
-
-    with jax.named_scope("end_sent"):
-        lax.fori_loop(0, 2 * LAYERS, sent, 0)
+    blocks = wb.at[0, :, pl.ds(0, 3)]
+    for i in range(LAYERS + 1):
+        pltpu.make_async_copy(blocks, blocks, ag_s.at[i]).wait()
     for j, dst in enumerate((pv, mv, vv)):
         pltpu.make_async_copy(dst, dst, out_sem.at[j]).wait()
 
@@ -754,26 +799,26 @@
             dma((2,)),
             dma((2,)),
             dma((2,)),
+            dma((2,)),
             dma((LAYERS, 2)),
-            dma((LAYERS, 2)),
-            dma((2 * LAYERS, 4)),
-            dma((2 * LAYERS, 4)),
+            dma((LAYERS + 1,)),
+            dma((2 * LAYERS + 1, 4)),
             dma((5,)),
             dma((5,)),
             dma((4,)),
             dma((4,)),
             dma((CHUNKS, 2)),
             dma((CHUNKS, 2)),
+            dma((4,)),
             dma((8,)),
+            dma((4,)),
             dma((8,)),
+            dma((4,)),
             dma((8,)),
+            dma((4,)),
             dma((8,)),
-            dma((8,)),
-            dma((8,)),
-            dma((8,)),
-            dma((8,)),
-            dma((CHUNKS, 2)),
-            dma((CHUNKS, 2)),
+            dma((2,)),
+            dma((1,)),
         ],
         compiler_params=pltpu.CompilerParams(
             collective_id=0, has_side_effects=True, vmem_limit_bytes=49200000

time: 147 us -> 146 us (level)
  no operation moved by 1% of the time
where the time goes in v4:
time: 146 us
  Pallas kernels  144 us (99%)
  between operations  2.09 us (1%)
    pallas_call x1, Pallas kernels, per_device(): pl.pallas_call(kernel, out_shape=shapes, in_specs=[hbm, smem, hbm, smem,...  141 us
    pallas_call x1, Pallas kernels, per_device(): pl.pallas_call(hand_over, out_shape=shapes, in_specs=[any_space] * 4, out...  3.02 us

profile of v4, /device:TPU:1, one launch (start us, length us, event | category | flops | bytes accessed | tf_op | source)
XLA Modules:
  0.0 145.7 jit_solution(5729709633591672064)
XLA Ops:
  1.9 140.6 %shard_map.120 = (f32[4,128,1024]{2,1,0:T(8,128)S(1)}, f32[4,128,1024]{2,1,0:T(8,128)S(1)}, f32[4,128,1024]{2,1,0:T(8,128)S(1)}, bf16[512,1024]{1,0:T(8,128)(2,1)S(1)}) custom-call(bf16[512,4096]{1,0:T(8,128)(2,1)} %tokens_hbm.1, s32[1]{0:T(128)S(6)} %copy.13.counts_ref, s32[512]{0:T(512)} %patch_hbm.1, f32[1,1]{1,0:T(1,128)} %bitcast.1.clip_ref, ...), custom_call_target="tpu_custom_call" | custom-call | tf_op jit(solution)/shard_map/pallas_call | solution.py:769
  142.5 3.0 %shard_map.121 = (f32[4,128,1024]{2,1,0:T(8,128)}, f32[4,128,1024]{2,1,0:T(8,128)}, f32[4,128,1024]{2,1,0:T(8,128)}, bf16[512,1024]{1,0:T(8,128)(2,1)}) custom-call(f32[4,128,1024]{2,1,0:T(8,128)S(1)} %get-tuple-element.8.p, f32[4,128,1024]{2,1,0:T(8,128)S(1)} %get-tuple-element.9.m, f32[4,128,1024]{2,1,0:T(8,128)S(1)} %get-tuple-element.10.v, ...), custom_call_target="tpu_custom_call" | custom-call | tf_op jit(solution)/shard_map/pallas_call | solution.py:837

commit v5 on v4

--- a/solution.py
+++ b/solution.py
@@ -553,14 +553,14 @@
             stream[k] = values.reshape(2, ROWS, HALF)
             mean = jnp.sum(values, axis=1, keepdims=True) * (1.0 / HALF)
             d = values - mean
+            xbuf[(s // 4 + 1) % 2, k, mine] = d.astype(BF).reshape(2, ROWS, HALF)
+            chip_copy(s).start()
+            core_copy(s).start()
             square = jnp.sum(d * d, axis=1, keepdims=True)
             lanes = lax.broadcasted_iota(jnp.int32, (2 * ROWS, 128), 1)
             cols = jnp.where(lanes == 0, mean, jnp.where(lanes == 1, square, 0.0))
             statbuf[s, 0] = cols.T[0:2, :]
-            xbuf[(s // 4 + 1) % 2, k, mine] = d.astype(BF).reshape(2, ROWS, HALF)
             start_all(stat_copies(s))
-            chip_copy(s).start()
-            core_copy(s).start()
 
     def give_rest(s):
         k = s % 4

time: 146 us -> 146 us (level)
  no operation moved by 1% of the time
where the time goes in v5:
time: 146 us; the launch traced here: 145 us
  Pallas kernels  143 us (98%)
  between operations  2.09 us (1%)
    pallas_call x1, Pallas kernels, per_device(): pl.pallas_call(kernel, out_shape=shapes, in_specs=[hbm, smem, hbm, smem,...  140 us
    pallas_call x1, Pallas kernels, per_device(): pl.pallas_call(hand_over, out_shape=shapes, in_specs=[any_space] * 4, out...  3.02 us

profile of v5, /device:TPU:1, one launch (start us, length us, event | category | flops | bytes accessed | tf_op | source)
XLA Modules:
  0.0 145.5 jit_solution(6729193328385249770)
XLA Ops:
  1.9 140.4 %shard_map.120 = (f32[4,128,1024]{2,1,0:T(8,128)S(1)}, f32[4,128,1024]{2,1,0:T(8,128)S(1)}, f32[4,128,1024]{2,1,0:T(8,128)S(1)}, bf16[512,1024]{1,0:T(8,128)(2,1)S(1)}) custom-call(bf16[512,4096]{1,0:T(8,128)(2,1)} %tokens_hbm.1, s32[1]{0:T(128)S(6)} %copy.13.counts_ref, s32[512]{0:T(512)} %patch_hbm.1, f32[1,1]{1,0:T(1,128)} %bitcast.1.clip_ref, ...), custom_call_target="tpu_custom_call" | custom-call | tf_op jit(solution)/shard_map/pallas_call | solution.py:769
  142.3 3.0 %shard_map.121 = (f32[4,128,1024]{2,1,0:T(8,128)}, f32[4,128,1024]{2,1,0:T(8,128)}, f32[4,128,1024]{2,1,0:T(8,128)}, bf16[512,1024]{1,0:T(8,128)(2,1)}) custom-call(f32[4,128,1024]{2,1,0:T(8,128)S(1)} %get-tuple-element.8.p, f32[4,128,1024]{2,1,0:T(8,128)S(1)} %get-tuple-element.9.m, f32[4,128,1024]{2,1,0:T(8,128)S(1)} %get-tuple-element.10.v, ...), custom_call_target="tpu_custom_call" | custom-call | tf_op jit(solution)/shard_map/pallas_call | solution.py:837
